TPU v7x, 32 devices: a whole 2x2x4 slice. The times are simulated.
32 devices in a mesh: gz: 2 (over x), gy: 4 (over y, core), gx: 4 (over z).
Axes of the slice: x: 2, y: 2, z: 4, core: 2. Of those that a mesh axis runs over, the one named last changes fastest.
Arguments:
- density: float32 [32, 64, 256], P('gx', 'gy', 'gz'), may hold values from 0.05 to 0.95
- spread: float32 [32, 64, 256], P('gx', 'gy', 'gz'), may hold values from 0.05 to 0.3
- sensitivities: float32 [9, 32, 64, 256], P(None, 'gx', 'gy', 'gz'), may hold values from -180 to 180, as said below
- violation: float32 [9], replicated, may hold values from -0.05 to 0.15
- multipliers_start: float32 [9], replicated, may hold values from 0.1 to 10
Outputs:
- new_density: float32 [32, 64, 256], P('gx', 'gy', 'gz')
- multipliers: float32 [9], replicated
Inputs may be any that keep to these rules, and one draw needn't show every extreme that they name: `sensitivities`: Real-valued, independent from voxel to voxel.
All inputs are finite; a program needn't handle non-finite values.
Results may differ from a plain program's by a relative error of at most 0.0003.
Values sent between devices are 32-bit elements; how exact they have to be, the bound alone decides.
A program may use at most 64 MiB of HBM per device.

v0:
```python
import functools
import math

import jax
import jax.numpy as jnp
from jax import lax
from jax.experimental import pallas as pl
from jax.experimental.pallas import tpu as pltpu
from jax.sharding import PartitionSpec as P

FIELDS = 9
ITERS = 3

RADIUS = 3.0
RAA = 1e-05
MOVE = 0.9
REG = 0.001
FLOOR = 0.2

W0 = RADIUS
W1 = RADIUS - 1.0
W2 = RADIUS - math.sqrt(2.0)
W3 = RADIUS - math.sqrt(3.0)

SUB, LANE = 8, 128
AXES = ("gz", "gy", "gx")
SUMS = FIELDS + FIELDS * (FIELDS + 1) // 2
ROWS = SUMS + FIELDS
MESH = pl.DeviceIdType.MESH
GROUP = 3


def plan(shape):
    total = math.prod(shape[a] for a in AXES)
    if total <= 32:
        return (AXES,)
    return tuple((a,) for a in AXES)


def offsets(axes, shape):
    out = [()]
    for a in axes:
        out = [o + (d,) for o in out for d in range(shape[a])]
    return [o for o in out if any(o)]


def steps():
    return [range(f, min(f + GROUP, FIELDS)) for f in range(0, FIELDS, GROUP)]


def body(shape, dims, dens_hbm, span_hbm, sens_ref, viol_hbm, lam0_hbm, out_hbm, lam_out,
         dens_ref, span_ref, out_ref, viol_ref, lam0_ref, pad, ypack, yrecv, cpack, crecv, zpack, zrecv, mid, invden, pp, qq, slope, scaled,
         acc, wide, lam, part, *rest):
    stages = plan(shape)
    recvs = rest[: len(stages)]
    load_sem, send_sem, recv_sem, sum_send, sum_recv, known = rest[len(stages):]
    nx, ny, nz = dims
    tiles = ny // SUB
    chunks = nx * tiles
    me = {a: lax.axis_index(a) for a in AXES}

    has = {}
    for a in AXES:
        has[a, -1] = me[a] > 0
        has[a, 0] = jnp.bool_(True)
        has[a, 1] = me[a] < shape[a] - 1

    def both(o):
        moved = [has[a, d] for a, d in zip(AXES, o) if d]
        return functools.reduce(jnp.logical_and, moved)

    def at(**moves):
        return {a: me[a] + d for a, d in moves.items()}

    plane = [(0, dy, dx) for dy in (-1, 0, 1) for dx in (-1, 0, 1) if dy or dx]
    barrier = pltpu.get_barrier_semaphore()
    near = shape["gz"] == 2 and shape["gy"] <= 4 and shape["gx"] <= 4
    if near:
        greeted = [(-1, 0, 0), (1, 0, 0)] + plane
        for o in greeted:
            @pl.when(both(o))
            def _(o=o):
                pl.semaphore_signal(barrier, inc=1, device_id=at(gz=o[0], gy=o[1], gx=o[2]),
                                    device_id_type=MESH)
        arrivals = sum(both(o).astype(jnp.int32) for o in greeted)
    else:
        partners = set()
        for axes in stages:
            for o in offsets(axes, shape):
                partners.add(tuple(dict(zip(axes, o)).get(a, 0) for a in AXES))
        for d in [(-1, 0, 0), (1, 0, 0)] + plane:
            o = tuple(d % shape[a] for a, d in zip(AXES, d))
            if any(o):
                partners.add(o)
        partners = sorted(partners)
        for o in partners:
            target = {a: lax.rem(me[a] + d, shape[a]) for a, d in zip(AXES, o)}
            pl.semaphore_signal(barrier, inc=1, device_id=target, device_id_type=MESH)
        arrivals = len(partners)

    load = pltpu.make_async_copy(
        sens_ref, pad.at[:, 1 : nx + 1, SUB : SUB + ny, :], load_sem.at[0]
    )
    load.start()
    small = [
        pltpu.make_async_copy(src, dst, load_sem.at[1 + i])
        for i, (src, dst) in enumerate([
            (span_hbm, span_ref), (dens_hbm, dens_ref), (viol_hbm, viol_ref), (lam0_hbm, lam0_ref)])
    ]
    for copy in small:
        copy.start()

    lane = lax.broadcasted_iota(jnp.int32, (SUB, LANE), 1)
    row = lax.broadcasted_iota(jnp.int32, (SUB, LANE), 0)
    zero = jnp.zeros((SUB, LANE), jnp.float32)

    for i, sx in enumerate((1, -1)):
        @pl.when(jnp.logical_not(has["gx", -sx]))
        def _(i=i):
            pad[:, i * (nx + 1), SUB : SUB + ny, :] = jnp.zeros((FIELDS, ny, LANE), jnp.float32)
    for i, sy in enumerate((1, -1)):
        @pl.when(jnp.logical_not(has["gy", -sy]))
        def _(i=i):
            yrecv[i] = jnp.zeros((FIELDS, nx, LANE), jnp.float32)
    for i, sz in enumerate((1, -1)):
        @pl.when(jnp.logical_not(has["gz", -sz]))
        def _(i=i):
            zrecv[i] = jnp.zeros(zrecv.shape[1:], jnp.float32)
    corners = [(sx, sy) for sx in (1, -1) for sy in (1, -1)]
    for i, (sx, sy) in enumerate(corners):
        @pl.when(jnp.logical_not(jnp.logical_and(has["gx", -sx], has["gy", -sy])))
        def _(i=i):
            crecv[i] = jnp.zeros((FIELDS, 1, LANE), jnp.float32)

    def count(a, index, extent):
        low = jnp.where(jnp.logical_and(me[a] == 0, index == 0), 0.0, 1.0)
        high = jnp.where(jnp.logical_and(me[a] == shape[a] - 1, index == extent - 1), 0.0, 1.0)
        return low + high
    cz = count("gz", lane, nz)
    for x in range(nx):
        cx = count("gx", jnp.full((SUB, LANE), x, jnp.int32), nx)
        for t in range(tiles):
            cy = count("gy", row + t * SUB, ny)
            den = W0 + W1 * (cx + cy + cz) + W2 * (cx * cy + cy * cz + cx * cz) + W3 * (cx * cy * cz)
            k = x * tiles + t
            invden[k] = 1.0 / den

    load.wait()

    for f in range(FIELDS):
        for i, y in enumerate((SUB + ny - 1, SUB)):
            for x in range(nx):
                ypack[i, f, x : x + 1, :] = pad[f, x + 1, y : y + 1, :]
        for i, (sx, sy) in enumerate(corners):
            x = nx if sx > 0 else 1
            y = SUB + ny - 1 if sy > 0 else SUB
            cpack[i, f] = pad[f, x, y : y + 1, :]

    pl.semaphore_wait(barrier, arrivals)

    groups = steps()
    count_of = len(groups)

    def moves_x(g):
        fields = pl.ds(groups[g][0], len(groups[g]))
        out = []
        for i, sx in enumerate((1, -1)):
            copy = pltpu.make_async_remote_copy(
                src_ref=pad.at[fields, nx if sx > 0 else 1, SUB : SUB + ny, :],
                dst_ref=pad.at[fields, 0 if sx > 0 else nx + 1, SUB : SUB + ny, :],
                send_sem=send_sem.at[6 + 4 * g + i], recv_sem=recv_sem.at[6 + 4 * g + i],
                device_id=at(gx=sx), device_id_type=MESH)
            out.append((has["gx", sx], has["gx", -sx], copy))
        return out

    moves_c, moves_y, moves_z = [], [], []
    for i, (sx, sy) in enumerate(corners):
        copy = pltpu.make_async_remote_copy(
            src_ref=cpack.at[i], dst_ref=crecv.at[i],
            send_sem=send_sem.at[2 + i], recv_sem=recv_sem.at[2 + i],
            device_id=at(gx=sx, gy=sy), device_id_type=MESH)
        moves_c.append((jnp.logical_and(has["gx", sx], has["gy", sy]),
                        jnp.logical_and(has["gx", -sx], has["gy", -sy]), copy))
    for i, sy in enumerate((1, -1)):
        copy = pltpu.make_async_remote_copy(
            src_ref=ypack.at[i], dst_ref=yrecv.at[i],
            send_sem=send_sem.at[i], recv_sem=recv_sem.at[i],
            device_id=at(gy=sy), device_id_type=MESH)
        moves_y.append((has["gy", sy], has["gy", -sy], copy))

    def start(moves):
        for send, _, copy in moves:
            pl.when(send)(copy.start)

    def receive(moves):
        for _, expected, copy in moves:
            pl.when(expected)(copy.wait_recv)

    xs = [moves_x(g) for g in range(count_of)]
    start(moves_c)
    start(xs[0])
    start(moves_y)
    for g in range(1, count_of):
        start(xs[g])
    receive(moves_c)
    receive(moves_y)

    ends = jnp.logical_or(lane == 0, lane == LANE - 1)

    def smooth(f, g):
        for i, y in enumerate((SUB - 1, SUB + ny)):
            for x in range(nx):
                pad[f, x + 1, y : y + 1, :] = yrecv[i, f, x : x + 1, :]
        for i, (sx, sy) in enumerate(corners):
            pad[f, 0 if sx > 0 else nx + 1, (SUB - 1 if sy > 0 else SUB + ny) : (SUB if sy > 0 else SUB + ny + 1), :] = crecv[i, f]
        packed = zero
        for t in range(tiles):
            y = SUB + t * SUB
            mids, sides = [], []
            for p in range(nx + 2):
                mids.append(pad[f, p, y : y + SUB, :])
                sides.append(pad[f, p, y - 1 : y - 1 + SUB, :] + pad[f, p, y + 1 : y + 1 + SUB, :])
            for x in range(nx):
                k = x * tiles + t
                near = sides[x + 1] + (mids[x] + mids[x + 2])
                far = sides[x] + sides[x + 2]
                s0 = W0 * mids[x + 1] + W1 * near + W2 * far
                s1 = W1 * mids[x + 1] + W2 * near + W3 * far
                up = pltpu.roll(s1, 1, 1)
                down = pltpu.roll(s1, LANE - 1, 1)
                mid[f, k] = s0 + jnp.where(lane == 0, 0.0, up) + jnp.where(lane == LANE - 1, 0.0, down)
                edge = jnp.where(lane == 0, up, down)
                if k:
                    edge = pltpu.roll(edge, 2 * k, 1)
                here = jnp.logical_or(lane == 2 * k, lane == (2 * k - 1) % LANE)
                packed = jnp.where(here, edge, packed)
        shift = (f - groups[g][0]) * (2 * chunks)
        return pltpu.roll(packed, shift, 1) if shift else packed

    even = (lane % 2) == 0
    for g in range(count_of):
        receive(xs[g])
        v = zero
        for f in groups[g]:
            v += smooth(f, g)
        zpack[0, g] = jnp.where(even, v, 0.0)
        zpack[1, g] = jnp.where(even, 0.0, v)
        zs = []
        for i, sz in enumerate((1, -1)):
            copy = pltpu.make_async_remote_copy(
                src_ref=zpack.at[i, g], dst_ref=zrecv.at[i, g],
                send_sem=send_sem.at[8 + 4 * g + i], recv_sem=recv_sem.at[8 + 4 * g + i],
                device_id=at(gz=sz), device_id_type=MESH)
            zs.append((has["gz", sz], has["gz", -sz], copy))
        start(zs)
        moves_z.append(zs)

    def piece(ref, k):
        x, t = divmod(k, tiles)
        return ref[x, t * SUB : (t + 1) * SUB, :]

    def rows(f, g):
        outer = zrecv[0, g] + zrecv[1, g]
        shift = (f - groups[g][0]) * (2 * chunks)
        total = zero
        for k in range(chunks):
            turn = (LANE - shift - 2 * k) % LANE
            edge = pltpu.roll(outer, turn, 1) if turn else outer
            r = (mid[f, k] + jnp.where(ends, edge, 0.0)) * invden[k]
            s = piece(span_ref, k)
            square = s * s
            gp = jnp.maximum(r, 0.0)
            gm = jnp.maximum(-r, 0.0)
            pp[f, k] = square * (1.001 * gp + 0.001 * gm + RAA)
            qq[f, k] = square * (0.001 * gp + 1.001 * gm + RAA)
            total += s * (1.002 * (gp + gm) + 2 * RAA)
        if f:
            acc[SUMS - 1 + f] = total

    for copy in small:
        copy.wait()
    for g in range(count_of):
        receive(moves_z[g])
        if near and g == 0:
            for o in plane:
                @pl.when(both(o))
                def _(o=o):
                    pl.semaphore_signal(known, inc=1, device_id=at(gy=o[1], gx=o[2]),
                                        device_id_type=MESH)
        for f in groups[g]:
            rows(f, g)
    total = zero
    for k in range(chunks):
        s = piece(span_ref, k)
        square = s * s
        pp[FIELDS, k] = square * (1.001 + RAA)
        qq[FIELDS, k] = square * (0.001 + RAA)
        total += s * (1.002 + 2 * RAA)
    acc[ROWS - 1] = total
    for k in range(FIELDS):
        lam[k] = jnp.full((SUB, LANE), lam0_ref[k], jnp.float32)

    def respond(k, weights):
        big_p, big_q = pp[0, k], qq[0, k]
        for j in range(FIELDS):
            big_p += weights[j] * pp[j + 1, k]
            big_q += weights[j] * qq[j + 1, k]
        s = piece(span_ref, k)
        d = piece(dens_ref, k)
        root_p = jnp.sqrt(big_p)
        root_q = jnp.sqrt(big_q)
        lower, upper = d - s, d + s
        moved = (root_p * lower + root_q * upper) / (root_p + root_q)
        low = jnp.maximum(0.0, d - MOVE * s)
        high = jnp.minimum(1.0, d + MOVE * s)
        return jnp.minimum(jnp.maximum(moved, low), high), big_p, big_q, lower, upper

    def flat(axes):
        index = 0
        for a in axes:
            index = index * shape[a] + me[a]
        return index

    def newton(it, carry):
        weights = [lam[j] for j in range(FIELDS)]
        grads = [zero] * FIELDS
        for k in range(chunks):
            moved, big_p, big_q, lower, upper = respond(k, weights)
            ia = 1.0 / (upper - moved)
            ib = 1.0 / (moved - lower)
            ia2, ib2 = ia * ia, ib * ib
            inv = 1.0 / (2.0 * big_p * (ia2 * ia) + 2.0 * big_q * (ib2 * ib))
            for j in range(FIELDS):
                p, q = pp[j + 1, k], qq[j + 1, k]
                grads[j] += p * ia + q * ib
                a = p * ia2 - q * ib2
                slope[j, k] = a
                scaled[j, k] = a * inv
        for j in range(FIELDS):
            acc[j] = grads[j]
        at_row = FIELDS
        for group in ((0, 1), (2, 3), (4, 5, 6, 7, 8)):
            sums = {(i, j): zero for i in group for j in range(i, FIELDS)}
            for k in range(chunks):
                right = {j: slope[j, k] for j in range(group[0], FIELDS)}
                for i in group:
                    left = scaled[i, k]
                    for j in range(i, FIELDS):
                        sums[i, j] += left * right[j]
            for key in sums:
                acc[at_row] = sums[key]
                at_row += 1

        packed = zero
        for r in range(ROWS):
            packed = jnp.where(lane == r, jnp.sum(acc[r], axis=1, keepdims=True), packed)
        value = jnp.sum(packed, axis=0, keepdims=True)
        for n, axes in enumerate(stages):
            size = math.prod(shape[a] for a in axes)
            part[it, n] = value
            recvs[n][it, flat(axes)] = value
            for o in sorted(offsets(axes, shape), key=lambda o: (-abs(o[-1] - 2), o), reverse=True):
                target = {a: lax.rem(me[a] + d, shape[a]) for a, d in zip(axes, o)}
                pltpu.make_async_remote_copy(
                    src_ref=part.at[it, n], dst_ref=recvs[n].at[it, flat(axes)],
                    send_sem=sum_send.at[it, n], recv_sem=sum_recv.at[it, n],
                    device_id=target, device_id_type=MESH).start()
            whole = recvs[n].at[it, pl.ds(0, size - 1)]
            pltpu.make_async_copy(whole, whole, sum_recv.at[it, n]).wait()
            values = [recvs[n][it, i] for i in range(size)]
            while len(values) > 1:
                values = [sum(values[i + 1 : i + 2], values[i]) for i in range(0, len(values), 2)]
            value = values[0]
        every = jnp.broadcast_to(value, (SUB, LANE))
        for g in range(wide.shape[0]):
            one = jnp.sum(jnp.where(lane == g * SUB + row, every, 0.0), axis=1, keepdims=True)
            wide[g] = jnp.broadcast_to(one, (SUB, LANE))

        def read(r):
            return jnp.broadcast_to(wide[r // SUB, r % SUB : r % SUB + 1, :], (SUB, LANE))
        b = [read(j) - (1.0 - viol_ref[j]) * read(SUMS + j) for j in range(FIELDS)]
        m = {}
        at_row = FIELDS
        for i in range(FIELDS):
            for j in range(i, FIELDS):
                m[i, j] = read(at_row)
                at_row += 1
        trace = m[0, 0]
        for i in range(1, FIELDS):
            trace += m[i, i]
        shift = REG * trace / FIELDS
        for i in range(FIELDS):
            m[i, i] += shift
        inverse = []
        for k in range(FIELDS):
            inverse.append(1.0 / m[k, k])
            for i in range(k + 1, FIELDS):
                factor = m[k, i] * inverse[k]
                for j in range(i, FIELDS):
                    m[i, j] -= factor * m[k, j]
                b[i] -= factor * b[k]
        delta = [None] * FIELDS
        for k in reversed(range(FIELDS)):
            v = b[k]
            for j in range(k + 1, FIELDS):
                v -= m[k, j] * delta[j]
            delta[k] = v * inverse[k]
        for k in range(FIELDS):
            lam[k] = jnp.maximum(weights[k] + delta[k], FLOOR * weights[k])
        return carry
    if near:
        pl.semaphore_wait(known, sum(both(o).astype(jnp.int32) for o in plane))
    lax.fori_loop(0, ITERS, newton, 0)

    weights = [lam[j] for j in range(FIELDS)]
    for k in range(chunks):
        x, t = divmod(k, tiles)
        out_ref[x, t * SUB : (t + 1) * SUB, :] = respond(k, weights)[0]
    result = pltpu.make_async_copy(out_ref, out_hbm, load_sem.at[0])
    result.start()
    for j in range(FIELDS):
        lam_out[j] = jnp.max(weights[j])

    for moves in [moves_c, moves_y] + xs + moves_z:
        for send, _, copy in moves:
            pl.when(send)(copy.wait_send)
    for it in range(ITERS):
        for n, axes in enumerate(stages):
            size = math.prod(shape[a] for a in axes)
            whole = recvs[n].at[it, pl.ds(0, size - 1)]
            pltpu.make_async_copy(whole, whole, sum_send.at[it, n]).wait()
    result.wait()


def finish(field_ref, lam_ref, field_out, lam_out, sem):
    copies = [pltpu.make_async_copy(field_ref, field_out, sem.at[0]),
              pltpu.make_async_copy(lam_ref, lam_out, sem.at[1])]
    for copy in copies:
        copy.start()
    for copy in copies:
        copy.wait()


def shards(shape, density, spread, sensitivities, violation, multipliers_start):
    nx, ny, nz = density.shape
    chunks = nx * ny // SUB
    groups = len(steps())
    stages = plan(shape)
    f32 = jnp.float32
    smem = pl.BlockSpec(memory_space=pltpu.SMEM)
    dma = pltpu.SemaphoreType.DMA
    hbm = pl.BlockSpec(memory_space=pltpu.HBM)
    anywhere = pl.BlockSpec(memory_space=pl.ANY)
    field, lam = pl.pallas_call(
        functools.partial(body, shape, (nx, ny, nz)),
        out_shape=(
            jax.ShapeDtypeStruct((nx, ny, nz), f32),
            jax.ShapeDtypeStruct((FIELDS,), f32),
        ),
        in_specs=[hbm] * 5,
        out_specs=(anywhere, smem),
        scratch_shapes=[
            pltpu.VMEM((nx, ny, nz), f32),
            pltpu.VMEM((nx, ny, nz), f32),
            pltpu.VMEM((nx, ny, nz), f32),
            pltpu.SMEM((FIELDS,), f32),
            pltpu.SMEM((FIELDS,), f32),
            pltpu.VMEM((FIELDS, nx + 2, ny + 2 * SUB, nz), f32),
            pltpu.VMEM((2, FIELDS, nx, nz), f32),
            pltpu.VMEM((2, FIELDS, nx, nz), f32),
            pltpu.VMEM((4, FIELDS, 1, nz), f32),
            pltpu.VMEM((4, FIELDS, 1, nz), f32),
            pltpu.VMEM((2, groups, SUB, LANE), f32),
            pltpu.VMEM((2, groups, SUB, LANE), f32),
            pltpu.VMEM((FIELDS, chunks, SUB, LANE), f32),
            pltpu.VMEM((chunks, SUB, LANE), f32),
            pltpu.VMEM((FIELDS + 1, chunks, SUB, LANE), f32),
            pltpu.VMEM((FIELDS + 1, chunks, SUB, LANE), f32),
            pltpu.VMEM((FIELDS, chunks, SUB, LANE), f32),
            pltpu.VMEM((FIELDS, chunks, SUB, LANE), f32),
            pltpu.VMEM((ROWS, SUB, LANE), f32),
            pltpu.VMEM((-(-ROWS // SUB), SUB, LANE), f32),
            pltpu.VMEM((FIELDS, SUB, LANE), f32),
            pltpu.VMEM((ITERS, len(stages), 1, LANE), f32),
        ] + [
            pltpu.VMEM((ITERS, math.prod(shape[a] for a in axes), 1, LANE), f32) for axes in stages
        ] + [
            dma((5,)), dma((6 + 4 * groups,)), dma((6 + 4 * groups,)),
            dma((ITERS, len(stages))), dma((ITERS, len(stages))), pltpu.SemaphoreType.REGULAR,
        ],
        compiler_params=pltpu.CompilerParams(
            collective_id=0, has_side_effects=True, vmem_limit_bytes=24 << 20),
        name="design_step",
    )(*[pltpu.with_memory_space_constraint(v, pltpu.HBM) for v in (density, spread, sensitivities, violation, multipliers_start)])
    return pl.pallas_call(
        finish,
        out_shape=(
            jax.ShapeDtypeStruct((nx, ny, nz), f32),
            jax.ShapeDtypeStruct((FIELDS,), f32),
        ),
        in_specs=[anywhere, anywhere],
        out_specs=(hbm, hbm),
        scratch_shapes=[dma((2,))],
        compiler_params=pltpu.CompilerParams(vmem_limit_bytes=1 << 20),
        name="finish",
    )(field, lam)


def solution(mesh):
    shape = {a: int(mesh.shape[a]) for a in AXES}
    return jax.shard_map(
        functools.partial(shards, shape),
        mesh=mesh,
        in_specs=(P("gx", "gy", "gz"), P("gx", "gy", "gz"), P(None, "gx", "gy", "gz"), P(), P()),
        out_specs=(P("gx", "gy", "gz"), P()),
        check_vma=False,
    )
```

profile of v0, /device:TPU:0, one launch (start us, length us, event | category | flops | bytes accessed | tf_op | source)
XLA Modules:
  0.0 30.6 jit_solution(2572600176714609593)
XLA Ops:
  0.6 29.3 %design_step.1 = (f32[8,16,128]{2,1,0:T(8,128)S(1)}, f32[9]{0:T(128)S(1)}) custom-call(f32[8,16,128]{2,1,0:T(8,128)} %dens_hbm.1, f32[8,16,128]{2,1,0:T(8,128)} %span_hbm.1, f32[9,8,16,128]{3,2,1,0:T(8,128)} %sens_ref.1, f32[9]{0:T(128)} %viol_hbm.1, f32[9]{0:T(128)} %lam0_hbm.1), custom_call_target="tpu_custom_call" | custom-call | tf_op jit(solution)/shard_map/design_step/pallas_call | solution.py:454
  30.0 0.7 %finish.1 = (f32[8,16,128]{2,1,0:T(8,128)}, f32[9]{0:T(128)}) custom-call(f32[8,16,128]{2,1,0:T(8,128)S(1)} %get-tuple-element.4.field_ref, f32[9]{0:T(128)S(1)} %get-tuple-element.5.lam_ref), custom_call_target="tpu_custom_call" | custom-call | tf_op jit(solution)/shard_map/finish/pallas_call | solution.py:495
where the time goes:
time: 30.8 us; the launch traced here: 30.6 us
  Pallas kernels  30 us (97%)
  between operations  0.64 us (2%)
    pallas_call x1, Pallas kernels, shards(): pl.pallas_call(functools.partial(body, shape, (nx, ny, nz)), out_shape=(j...  29.3 us
    pallas_call x1, Pallas kernels, shards(): pl.pallas_call(finish, out_shape=(jax.ShapeDtypeStruct((nx, ny, nz), f32)...  0.65 us

commit v1 on v0

--- a/solution.py
+++ b/solution.py
@@ -48,8 +48,8 @@
     return [range(f, min(f + GROUP, FIELDS)) for f in range(0, FIELDS, GROUP)]
 
 
-def body(shape, dims, dens_hbm, span_hbm, sens_ref, viol_hbm, lam0_hbm, out_hbm, lam_out,
-         dens_ref, span_ref, out_ref, viol_ref, lam0_ref, pad, ypack, yrecv, cpack, crecv, zpack, zrecv, mid, invden, pp, qq, slope, scaled,
+def body(shape, dims, dens_hbm, span_hbm, sens_ref, viol_hbm, lam0_hbm, out_ref, lam_out,
+         dens_ref, span_ref, viol_ref, lam0_ref, pad, ypack, yrecv, cpack, crecv, zpack, zrecv, mid, invden, pp, qq, slope, scaled,
          acc, wide, lam, part, *rest):
     stages = plan(shape)
     recvs = rest[: len(stages)]
@@ -416,10 +416,10 @@
     for k in range(chunks):
         x, t = divmod(k, tiles)
         out_ref[x, t * SUB : (t + 1) * SUB, :] = respond(k, weights)[0]
-    result = pltpu.make_async_copy(out_ref, out_hbm, load_sem.at[0])
-    result.start()
+    final = zero
     for j in range(FIELDS):
-        lam_out[j] = jnp.max(weights[j])
+        final = jnp.where(lane == j, weights[j], final)
+    lam_out[...] = final
 
     for moves in [moves_c, moves_y] + xs + moves_z:
         for send, _, copy in moves:
@@ -429,16 +429,16 @@
             size = math.prod(shape[a] for a in axes)
             whole = recvs[n].at[it, pl.ds(0, size - 1)]
             pltpu.make_async_copy(whole, whole, sum_send.at[it, n]).wait()
-    result.wait()
-
-
-def finish(field_ref, lam_ref, field_out, lam_out, sem):
-    copies = [pltpu.make_async_copy(field_ref, field_out, sem.at[0]),
-              pltpu.make_async_copy(lam_ref, lam_out, sem.at[1])]
-    for copy in copies:
-        copy.start()
-    for copy in copies:
-        copy.wait()
+
+
+def finish(field_ref, lam_ref, field_out, lam_out, row, sem):
+    whole = pltpu.make_async_copy(field_ref, field_out, sem.at[0])
+    whole.start()
+    row[...] = lam_ref[0, :FIELDS]
+    short = pltpu.make_async_copy(row, lam_out, sem.at[1])
+    short.start()
+    whole.wait()
+    short.wait()
 
 
 def shards(shape, density, spread, sensitivities, violation, multipliers_start):
@@ -447,20 +447,18 @@
     groups = len(steps())
     stages = plan(shape)
     f32 = jnp.float32
-    smem = pl.BlockSpec(memory_space=pltpu.SMEM)
+    vmem = pl.BlockSpec(memory_space=pltpu.VMEM)
     dma = pltpu.SemaphoreType.DMA
     hbm = pl.BlockSpec(memory_space=pltpu.HBM)
-    anywhere = pl.BlockSpec(memory_space=pl.ANY)
     field, lam = pl.pallas_call(
         functools.partial(body, shape, (nx, ny, nz)),
         out_shape=(
-            jax.ShapeDtypeStruct((nx, ny, nz), f32),
-            jax.ShapeDtypeStruct((FIELDS,), f32),
+            pltpu.VMEM((nx, ny, nz), f32),
+            pltpu.VMEM((SUB, LANE), f32),
         ),
         in_specs=[hbm] * 5,
-        out_specs=(anywhere, smem),
+        out_specs=(vmem, vmem),
         scratch_shapes=[
-            pltpu.VMEM((nx, ny, nz), f32),
             pltpu.VMEM((nx, ny, nz), f32),
             pltpu.VMEM((nx, ny, nz), f32),
             pltpu.SMEM((FIELDS,), f32),
@@ -498,9 +496,9 @@
             jax.ShapeDtypeStruct((nx, ny, nz), f32),
             jax.ShapeDtypeStruct((FIELDS,), f32),
         ),
-        in_specs=[anywhere, anywhere],
+        in_specs=[vmem, vmem],
         out_specs=(hbm, hbm),
-        scratch_shapes=[dma((2,))],
+        scratch_shapes=[pltpu.VMEM((FIELDS,), f32), dma((2,))],
         compiler_params=pltpu.CompilerParams(vmem_limit_bytes=1 << 20),
         name="finish",
     )(field, lam)

time: 30.8 us -> 29.9 us (0.971)
  Pallas kernels: 30 us -> 29.2 us
    pallas_call x1, Pallas kernels: 29.3 us -> 28.5 us  [shards(): pl.pallas_call(functools.partial(body, shape, (nx, ny, nz)), out_shape=(p...]
where the time goes in v1:
time: 29.9 us; the launch traced here: 29.8 us
  Pallas kernels  29.2 us (98%)
  between operations  0.64 us (2%)
    pallas_call x1, Pallas kernels, shards(): pl.pallas_call(functools.partial(body, shape, (nx, ny, nz)), out_shape=(p...  28.5 us
    pallas_call x1, Pallas kernels, shards(): pl.pallas_call(finish, out_shape=(jax.ShapeDtypeStruct((nx, ny, nz), f32)...  0.65 us

profile of v1, /device:TPU:0, one launch (start us, length us, event | category | flops | bytes accessed | tf_op | source)
XLA Modules:
  0.0 29.8 jit_solution(11859677307634017927)
XLA Ops:
  0.6 28.5 %design_step.1 = (f32[8,16,128]{2,1,0:T(8,128)S(1)}, f32[8,128]{1,0:T(8,128)S(1)}) custom-call(f32[8,16,128]{2,1,0:T(8,128)} %dens_hbm.1, f32[8,16,128]{2,1,0:T(8,128)} %span_hbm.1, f32[9,8,16,128]{3,2,1,0:T(8,128)} %sens_ref.1, f32[9]{0:T(128)} %viol_hbm.1, f32[9]{0:T(128)} %lam0_hbm.1), custom_call_target="tpu_custom_call" | custom-call | tf_op jit(solution)/shard_map/design_step/pallas_call | solution.py:453
  29.1 0.7 %finish.1 = (f32[8,16,128]{2,1,0:T(8,128)}, f32[9]{0:T(128)}) custom-call(f32[8,16,128]{2,1,0:T(8,128)S(1)} %get-tuple-element.4.field_ref, f32[8,128]{1,0:T(8,128)S(1)} %get-tuple-element.5.lam_ref), custom_call_target="tpu_custom_call" | custom-call | tf_op jit(solution)/shard_map/finish/pallas_call | solution.py:493

commit v2 on v1

v2 whole, which is shorter than its diff:
```python
import functools
import math

import jax
import jax.numpy as jnp
from jax import lax
from jax.experimental import pallas as pl
from jax.experimental.pallas import tpu as pltpu
from jax.sharding import PartitionSpec as P

FIELDS = 9
ITERS = 3

RADIUS = 3.0
RAA = 1e-05
MOVE = 0.9
REG = 0.001
FLOOR = 0.2

W0 = RADIUS
W1 = RADIUS - 1.0
W2 = RADIUS - math.sqrt(2.0)
W3 = RADIUS - math.sqrt(3.0)

SUB, LANE = 8, 128
AXES = ("gz", "gy", "gx")
SUMS = FIELDS + FIELDS * (FIELDS + 1) // 2
ROWS = SUMS + FIELDS
MESH = pl.DeviceIdType.MESH
GROUP = 3


def plan(shape):
    total = math.prod(shape[a] for a in AXES)
    if total <= 32:
        return (AXES,)
    return tuple((a,) for a in AXES)


def offsets(axes, shape):
    out = [()]
    for a in axes:
        out = [o + (d,) for o in out for d in range(shape[a])]
    return [o for o in out if any(o)]


def steps():
    return [range(f, min(f + GROUP, FIELDS)) for f in range(0, FIELDS, GROUP)]


def body(shape, dims, dens_hbm, span_hbm, sens_ref, viol_hbm, lam0_hbm, out_ref, lam_out,
         dens_ref, span_ref, viol_ref, lam0_ref, pad, xpad, ypack, yrecv, cpack, crecv, ycorr,
         zpack, zrecv, xzpack, xzrecv, yzpack, yzrecv, czrecv, around, mid, invden, pp, qq, slope, scaled,
         acc, wide, lam, part, *rest):
    stages = plan(shape)
    recvs = rest[: len(stages)]
    load_sem, send_sem, recv_sem, zsend_sem, zrecv_sem, sum_send, sum_recv, known = rest[len(stages):]
    nx, ny, nz = dims
    tiles = ny // SUB
    chunks = nx * tiles
    slots = 2 * chunks
    wide_x = 2 * tiles
    groups = steps()
    count_of = len(groups)
    me = {a: lax.axis_index(a) for a in AXES}

    has = {}
    for a in AXES:
        has[a, -1] = me[a] > 0
        has[a, 0] = jnp.bool_(True)
        has[a, 1] = me[a] < shape[a] - 1

    def both(o):
        moved = [has[a, d] for a, d in zip(AXES, o) if d]
        return functools.reduce(jnp.logical_and, moved)

    def at(**moves):
        return {a: me[a] + d for a, d in moves.items()}

    signs = (-1, 0, 1)
    plane = [(0, dy, dx) for dy in signs for dx in signs if dy or dx]
    ring = [(dz, dy, dx) for dz in signs for dy in signs for dx in signs if dz or dy or dx]
    barrier = pltpu.get_barrier_semaphore()
    near = shape["gz"] == 2 and shape["gy"] <= 4 and shape["gx"] <= 4
    if near:
        for o in ring:
            @pl.when(both(o))
            def _(o=o):
                pl.semaphore_signal(barrier, inc=1, device_id=at(gz=o[0], gy=o[1], gx=o[2]),
                                    device_id_type=MESH)
        arrivals = sum(both(o).astype(jnp.int32) for o in ring)
    else:
        partners = set()
        for axes in stages:
            for o in offsets(axes, shape):
                partners.add(tuple(dict(zip(axes, o)).get(a, 0) for a in AXES))
        for d in ring:
            o = tuple(d % shape[a] for a, d in zip(AXES, d))
            if any(o):
                partners.add(o)
        partners = sorted(partners)
        for o in partners:
            target = {a: lax.rem(me[a] + d, shape[a]) for a, d in zip(AXES, o)}
            pl.semaphore_signal(barrier, inc=1, device_id=target, device_id_type=MESH)
        arrivals = len(partners)

    load = pltpu.make_async_copy(
        sens_ref, pad.at[:, :, SUB : SUB + ny, :], load_sem.at[0]
    )
    load.start()
    small = [
        pltpu.make_async_copy(src, dst, load_sem.at[1 + i])
        for i, (src, dst) in enumerate([
            (span_hbm, span_ref), (dens_hbm, dens_ref), (viol_hbm, viol_ref), (lam0_hbm, lam0_ref)])
    ]
    for copy in small:
        copy.start()

    lane = lax.broadcasted_iota(jnp.int32, (SUB, LANE), 1)
    row = lax.broadcasted_iota(jnp.int32, (SUB, LANE), 0)
    zero = jnp.zeros((SUB, LANE), jnp.float32)
    slot = lane % slots
    x_of = slot // wide_x
    t_of = (slot % wide_x) // 2
    odd = (lane % 2) == 1
    ends = jnp.logical_or(lane == 0, lane == LANE - 1)

    corners = [(sx, sy) for sx in (1, -1) for sy in (1, -1)]
    line = jnp.zeros((1, LANE), jnp.float32)
    for f in range(FIELDS):
        for x in range(nx):
            pad[f, x, SUB - 1 : SUB, :] = line
            pad[f, x, SUB + ny : SUB + ny + 1, :] = line
        for i in range(2):
            xpad[i, f, SUB - 1 : SUB, :] = line
            xpad[i, f, SUB + ny : SUB + ny + 1, :] = line
    for i, sx in enumerate((1, -1)):
        @pl.when(jnp.logical_not(has["gx", -sx]))
        def _(i=i):
            xpad[i, :, SUB : SUB + ny, :] = jnp.zeros((FIELDS, ny, LANE), jnp.float32)
    for i, sy in enumerate((1, -1)):
        @pl.when(jnp.logical_not(has["gy", -sy]))
        def _(i=i):
            yrecv[i] = jnp.zeros((FIELDS, nx, LANE), jnp.float32)
    for i, (sx, sy) in enumerate(corners):
        @pl.when(jnp.logical_not(jnp.logical_and(has["gx", -sx], has["gy", -sy])))
        def _(i=i):
            crecv[i] = jnp.zeros((FIELDS, 1, LANE), jnp.float32)
    for i, sz in enumerate((1, -1)):
        @pl.when(jnp.logical_not(has["gz", -sz]))
        def _(i=i):
            zrecv[i] = jnp.zeros(zrecv.shape[1:], jnp.float32)
        for n, sx in enumerate((1, -1)):
            @pl.when(jnp.logical_not(jnp.logical_and(has["gz", -sz], has["gx", -sx])))
            def _(i=i, n=n):
                xzrecv[i, n] = zero
        for n, sy in enumerate((1, -1)):
            @pl.when(jnp.logical_not(jnp.logical_and(has["gz", -sz], has["gy", -sy])))
            def _(i=i, n=n):
                yzrecv[i, n] = zero
        for n, (sx, sy) in enumerate(corners):
            @pl.when(jnp.logical_not(both((-sz, -sy, -sx))))
            def _(i=i, n=n):
                czrecv[i, n] = zero

    def count(a, index, extent):
        low = jnp.where(jnp.logical_and(me[a] == 0, index == 0), 0.0, 1.0)
        high = jnp.where(jnp.logical_and(me[a] == shape[a] - 1, index == extent - 1), 0.0, 1.0)
        return low + high
    cz = count("gz", lane, nz)
    for x in range(nx):
        cx = count("gx", jnp.full((SUB, LANE), x, jnp.int32), nx)
        for t in range(tiles):
            cy = count("gy", row + t * SUB, ny)
            den = W0 + W1 * (cx + cy + cz) + W2 * (cx * cy + cy * cz + cx * cz) + W3 * (cx * cy * cz)
            k = x * tiles + t
            invden[k] = 1.0 / den

    load.wait()

    def turned(value, shift, axis=1):
        shift %= value.shape[axis]
        return pltpu.roll(value, shift, axis) if shift else value

    def place(packed, value, k, j):
        here = lane // 2 == k + j * chunks
        return jnp.where(here, turned(value, 2 * k + 1 + j * slots), packed)

    edges = []
    for g, fields in enumerate(groups):
        packed = zero
        for j, f in enumerate(fields):
            for k in range(chunks):
                x, t = divmod(k, tiles)
                packed = place(packed, pad[f, x, SUB + t * SUB : 2 * SUB + t * SUB, :], k, j)
        zpack[g] = packed
        edges.append(packed)
    for n, x in enumerate((nx - 1, 0)):
        packed = zero
        for g in range(count_of):
            packed = jnp.where(x_of == g, turned(edges[g], (g - x) * wide_x), packed)
        xzpack[n] = packed
    for n, y in enumerate((SUB - 1, 0)):
        packed = zero
        for g in range(count_of):
            packed = jnp.where(row == g, jnp.broadcast_to(edges[g][y : y + 1, :], (SUB, LANE)), packed)
        yzpack[n] = packed
    for f in range(FIELDS):
        for i, y in enumerate((SUB + ny - 1, SUB)):
            for x in range(nx):
                ypack[i, f, x : x + 1, :] = pad[f, x, y : y + 1, :]
        for i, (sx, sy) in enumerate(corners):
            x = nx - 1 if sx > 0 else 0
            y = SUB + ny - 1 if sy > 0 else SUB
            cpack[i, f] = pad[f, x, y : y + 1, :]

    pl.semaphore_wait(barrier, arrivals)

    def remote(src, dst, sends, recvs_, index, **moves):
        copy = pltpu.make_async_remote_copy(
            src_ref=src, dst_ref=dst, send_sem=sends.at[index], recv_sem=recvs_.at[index],
            device_id=at(**moves), device_id_type=MESH)
        there = functools.reduce(jnp.logical_and, [has[a, d] for a, d in moves.items()])
        back = functools.reduce(jnp.logical_and, [has[a, -d] for a, d in moves.items()])
        return there, back, copy

    def moves_x(g):
        fields = pl.ds(groups[g][0], len(groups[g]))
        return [
            remote(pad.at[fields, nx - 1 if sx > 0 else 0, SUB : SUB + ny, :],
                   xpad.at[i, fields, SUB : SUB + ny, :], send_sem, recv_sem, 6 + 2 * g + i, gx=sx)
            for i, sx in enumerate((1, -1))
        ]

    moves_c = [remote(cpack.at[i], crecv.at[i], send_sem, recv_sem, 2 + i, gx=sx, gy=sy)
               for i, (sx, sy) in enumerate(corners)]
    moves_y = [remote(ypack.at[i], yrecv.at[i], send_sem, recv_sem, i, gy=sy)
               for i, sy in enumerate((1, -1))]
    moves_z = []
    for i, sz in enumerate((1, -1)):
        first = 0 if shape["gz"] == 2 else 9 * i
        for n, (sx, sy) in enumerate(corners):
            moves_z.append(remote(yzpack.at[n % 2], czrecv.at[i, n], zsend_sem, zrecv_sem, first + 5 + n,
                                  gz=sz, gx=sx, gy=sy))
        for n, sx in enumerate((1, -1)):
            moves_z.append(remote(xzpack.at[n], xzrecv.at[i, n], zsend_sem, zrecv_sem, first + 1 + n,
                                  gz=sz, gx=sx))
        for n, sy in enumerate((1, -1)):
            moves_z.append(remote(yzpack.at[n], yzrecv.at[i, n], zsend_sem, zrecv_sem, first + 3 + n,
                                  gz=sz, gy=sy))
        moves_z.append(remote(zpack, zrecv.at[i], zsend_sem, zrecv_sem, first, gz=sz))

    def start(moves):
        for send, _, copy in moves:
            pl.when(send)(copy.start)

    def receive(moves):
        for _, expected, copy in moves:
            pl.when(expected)(copy.wait_recv)

    xs = [moves_x(g) for g in range(count_of)]
    start(moves_z)
    start(moves_c)
    start(xs[0])
    start(moves_y)
    for g in range(1, count_of):
        start(xs[g])

    def along(s0, s1):
        up = jnp.where(lane == 0, 0.0, pltpu.roll(s1, 1, 1))
        down = jnp.where(lane == LANE - 1, 0.0, pltpu.roll(s1, LANE - 1, 1))
        return s0 + up + down

    for f in range(FIELDS):
        for t in range(tiles):
            y = SUB + t * SUB
            mids, sides = [None], [None]
            for x in range(nx):
                mids.append(pad[f, x, y : y + SUB, :])
                sides.append(pad[f, x, y - 1 : y - 1 + SUB, :] + pad[f, x, y + 1 : y + 1 + SUB, :])
            mids.append(None)
            sides.append(None)
            for x in range(nx):
                next_to = [v for v in (mids[x], mids[x + 2]) if v is not None]
                beyond = [v for v in (sides[x], sides[x + 2]) if v is not None]
                close = sides[x + 1] + sum(next_to[1:], next_to[0])
                far = sum(beyond[1:], beyond[0])
                s0 = W0 * mids[x + 1] + W1 * close + W2 * far
                s1 = W1 * mids[x + 1] + W2 * close + W3 * far
                mid[f, x * tiles + t] = along(s0, s1)

    def piece(ref, k):
        x, t = divmod(k, tiles)
        return ref[x, t * SUB : (t + 1) * SUB, :]

    for copy in small:
        copy.wait()
    for n, ref in enumerate((span_ref, dens_ref, invden)):
        packed = zero
        for k in range(chunks):
            value = ref[k] if n == 2 else piece(ref, k)
            for j in range(LANE // slots):
                packed = place(packed, value, k, j)
        around[n] = packed
    for k in range(FIELDS):
        lam[k] = jnp.full((SUB, LANE), lam0_ref[k], jnp.float32)
    total = zero
    for k in range(chunks):
        s = piece(span_ref, k)
        square = s * s
        pp[FIELDS, k] = square * (1.001 + RAA)
        qq[FIELDS, k] = square * (0.001 + RAA)
        total += s * (1.002 + 2 * RAA)
    acc[ROWS - 1] = total

    receive(moves_c)
    receive(moves_y)
    x_row = lax.broadcasted_iota(jnp.int32, (nx, LANE), 0)
    x_lane = lax.broadcasted_iota(jnp.int32, (nx, LANE), 1)
    for i in range(2):
        for f in range(FIELDS):
            h = yrecv[i, f]
            low = jnp.broadcast_to(crecv[i, f], (nx, LANE))
            high = jnp.broadcast_to(crecv[2 + i, f], (nx, LANE))
            pair = jnp.where(x_row == 0, low, pltpu.roll(h, 1, 0)) + jnp.where(x_row == nx - 1, high, pltpu.roll(h, nx - 1, 0))
            s0 = W1 * h + W2 * pair
            s1 = W2 * h + W3 * pair
            up = jnp.where(x_lane == 0, 0.0, pltpu.roll(s1, 1, 1))
            down = jnp.where(x_lane == LANE - 1, 0.0, pltpu.roll(s1, LANE - 1, 1))
            ycorr[i, f] = s0 + up + down

    def grown(r, s):
        gp = jnp.maximum(r, 0.0)
        gm = jnp.maximum(-r, 0.0)
        square = s * s
        p = square * (1.001 * gp + 0.001 * gm + RAA)
        q = square * (0.001 * gp + 1.001 * gm + RAA)
        return p, q, s * (1.002 * (gp + gm) + 2 * RAA)

    def rows(f, j, packed):
        total = zero
        for k in range(chunks):
            x, t = divmod(k, tiles)
            value = mid[f, k]
            if t == 0:
                value += jnp.where(row == 0, jnp.broadcast_to(ycorr[0, f, x : x + 1, :], (SUB, LANE)), 0.0)
            if t == tiles - 1:
                value += jnp.where(row == SUB - 1, jnp.broadcast_to(ycorr[1, f, x : x + 1, :], (SUB, LANE)), 0.0)
            for i in range(2):
                if x == (0, nx - 1)[i]:
                    y = SUB + t * SUB
                    h = xpad[i, f, y : y + SUB, :]
                    pair = xpad[i, f, y - 1 : y - 1 + SUB, :] + xpad[i, f, y + 1 : y + 1 + SUB, :]
                    value += along(W1 * h + W2 * pair, W2 * h + W3 * pair)
            packed = place(packed, value, k, j)
            pp[f, k], qq[f, k], base = grown(value * invden[k], piece(span_ref, k))
            total += base
        if f:
            acc[SUMS - 1 + f] = total
        return packed

    inner = []
    for g, fields in enumerate(groups):
        receive(xs[g])
        if near and g == 0:
            for o in plane:
                @pl.when(both(o))
                def _(o=o):
                    pl.semaphore_signal(known, inc=1, device_id=at(gy=o[1], gx=o[2]),
                                        device_id_type=MESH)
        packed = zero
        for j, f in enumerate(fields):
            packed = rows(f, j, packed)
        inner.append(packed)

    def respond(k, weights):
        big_p, big_q = pp[0, k], qq[0, k]
        for j in range(FIELDS):
            big_p += weights[j] * pp[j + 1, k]
            big_q += weights[j] * qq[j + 1, k]
        s = around[0] if k == chunks else piece(span_ref, k)
        d = around[1] if k == chunks else piece(dens_ref, k)
        root_p = jnp.sqrt(big_p)
        root_q = jnp.sqrt(big_q)
        lower, upper = d - s, d + s
        moved = (root_p * lower + root_q * upper) / (root_p + root_q)
        low = jnp.maximum(0.0, d - MOVE * s)
        high = jnp.minimum(1.0, d + MOVE * s)
        return jnp.minimum(jnp.maximum(moved, low), high), big_p, big_q, lower, upper

    def terms(k, weights):
        moved, big_p, big_q, lower, upper = respond(k, weights)
        ia = 1.0 / (upper - moved)
        ib = 1.0 / (moved - lower)
        ia2, ib2 = ia * ia, ib * ib
        inv = 1.0 / (2.0 * big_p * (ia2 * ia) + 2.0 * big_q * (ib2 * ib))
        grads, slopes, ratios = [], [], []
        for j in range(FIELDS):
            p, q = pp[j + 1, k], qq[j + 1, k]
            grads.append(p * ia + q * ib)
            a = p * ia2 - q * ib2
            slopes.append(a)
            ratios.append(a * inv)
        return grads, slopes, ratios

    def main_sums(weights):
        grads = [zero] * FIELDS
        for k in range(chunks):
            more, slopes, ratios = terms(k, weights)
            for j in range(FIELDS):
                grads[j] += more[j]
                slope[j, k] = slopes[j]
                scaled[j, k] = ratios[j]
        for j in range(FIELDS):
            acc[j] = grads[j]
        at_row = FIELDS
        for group in ((0, 1), (2, 3), (4, 5, 6, 7, 8)):
            sums = {(i, j): zero for i in group for j in range(i, FIELDS)}
            for k in range(chunks):
                right = {j: slope[j, k] for j in range(group[0], FIELDS)}
                for i in group:
                    left = scaled[i, k]
                    for j in range(i, FIELDS):
                        sums[i, j] += left * right[j]
            for key in sums:
                acc[at_row] = sums[key]
                at_row += 1

    def combined(ref, *index):
        return jnp.where(odd, pltpu.roll(ref[(0,) + index], 1, 1), pltpu.roll(ref[(1,) + index], LANE - 1, 1))

    def outer_edges():
        last_x, last_t = wide_x * (nx - 1), 2 * (tiles - 1)
        yz = [combined(yzrecv, n) for n in range(2)]
        xz = [combined(xzrecv, n) for n in range(2)]
        cz_ = [combined(czrecv, n) for n in range(4)]

        def pick(value, g, shift):
            return turned(jnp.broadcast_to(value[g : g + 1, :], (SUB, LANE)), shift)

        def beside(c, first, final):
            down = pltpu.roll(c, 1, 0)
            up = pltpu.roll(c, SUB - 1, 0)
            before = jnp.where(row == 0, jnp.where(t_of == 0, first, turned(down, 2)), down)
            after = jnp.where(row == SUB - 1, jnp.where(t_of == tiles - 1, final, turned(up, LANE - 2)), up)
            return before + after

        out = []
        for g in range(count_of):
            c = combined(zrecv, g)
            s = beside(c, pick(yz[0], g, -last_t), pick(yz[1], g, last_t))
            c_low = turned(xz[0], -wide_x * g)
            c_high = turned(xz[1], last_x - wide_x * g)
            s_low = beside(c_low, pick(cz_[0], g, -last_x - last_t), pick(cz_[1], g, -last_x + last_t))
            s_high = beside(c_high, pick(cz_[2], g, last_x - last_t), pick(cz_[3], g, last_x + last_t))

            def pair(own, low, high):
                return (jnp.where(x_of == 0, low, turned(own, wide_x))
                        + jnp.where(x_of == nx - 1, high, turned(own, -wide_x)))
            out.append(W1 * c + W2 * (s + pair(c, c_low, c_high)) + W3 * pair(s, s_low, s_high))
        return out

    def edge_rows():
        outer = outer_edges()
        s = around[0]
        bases = []
        for g, fields in enumerate(groups):
            p, q, base = grown((inner[g] + outer[g]) * around[2], s)
            for j, f in enumerate(fields):
                pp[f, chunks] = turned(p, -j * slots)
                qq[f, chunks] = turned(q, -j * slots)
                bases.append(turned(base, -j * slots))
        pp[FIELDS, chunks] = s * s * (1.001 + RAA)
        qq[FIELDS, chunks] = s * s * (0.001 + RAA)
        return bases[1:] + [s * (1.002 + 2 * RAA)]

    def edge_sums(weights, bases):
        grads, slopes, ratios = terms(chunks, weights)
        more = grads + [ratios[i] * slopes[j] for i in range(FIELDS) for j in range(i, FIELDS)] + bases
        for r in range(ROWS):
            acc[r] = jnp.where(ends, 0.0, acc[r]) + jnp.where(lane < slots, more[r], 0.0)

    def repair():
        for f in range(FIELDS):
            p, q = pp[f, chunks], qq[f, chunks]
            for k in range(chunks):
                pp[f, k] = jnp.where(ends, turned(p, -2 * k - 1), pp[f, k])
                qq[f, k] = jnp.where(ends, turned(q, -2 * k - 1), qq[f, k])

    def flat(axes):
        index = 0
        for a in axes:
            index = index * shape[a] + me[a]
        return index

    def exchange(it, meanwhile):
        packed = zero
        for r in range(ROWS):
            packed = jnp.where(lane == r, jnp.sum(acc[r], axis=1, keepdims=True), packed)
        value = jnp.sum(packed, axis=0, keepdims=True)
        for n, axes in enumerate(stages):
            size = math.prod(shape[a] for a in axes)
            part[it, n] = value
            recvs[n][it, flat(axes)] = value
            for o in sorted(offsets(axes, shape), key=lambda o: (-abs(o[-1] - 2), o), reverse=True):
                target = {a: lax.rem(me[a] + d, shape[a]) for a, d in zip(axes, o)}
                pltpu.make_async_remote_copy(
                    src_ref=part.at[it, n], dst_ref=recvs[n].at[it, flat(axes)],
                    send_sem=sum_send.at[it, n], recv_sem=sum_recv.at[it, n],
                    device_id=target, device_id_type=MESH).start()
            if n == 0:
                meanwhile()
            whole = recvs[n].at[it, pl.ds(0, size - 1)]
            pltpu.make_async_copy(whole, whole, sum_recv.at[it, n]).wait()
            values = [recvs[n][it, i] for i in range(size)]
            while len(values) > 1:
                values = [sum(values[i + 1 : i + 2], values[i]) for i in range(0, len(values), 2)]
            value = values[0]
        every = jnp.broadcast_to(value, (SUB, LANE))
        for g in range(wide.shape[0]):
            one = jnp.sum(jnp.where(lane == g * SUB + row, every, 0.0), axis=1, keepdims=True)
            wide[g] = jnp.broadcast_to(one, (SUB, LANE))

    def solve(weights):
        def read(r):
            return jnp.broadcast_to(wide[r // SUB, r % SUB : r % SUB + 1, :], (SUB, LANE))
        b = [read(j) - (1.0 - viol_ref[j]) * read(SUMS + j) for j in range(FIELDS)]
        m = {}
        at_row = FIELDS
        for i in range(FIELDS):
            for j in range(i, FIELDS):
                m[i, j] = read(at_row)
                at_row += 1
        trace = m[0, 0]
        for i in range(1, FIELDS):
            trace += m[i, i]
        shift = REG * trace / FIELDS
        for i in range(FIELDS):
            m[i, i] += shift
        inverse = []
        for k in range(FIELDS):
            inverse.append(1.0 / m[k, k])
            for i in range(k + 1, FIELDS):
                factor = m[k, i] * inverse[k]
                for j in range(i, FIELDS):
                    m[i, j] -= factor * m[k, j]
                b[i] -= factor * b[k]
        delta = [None] * FIELDS
        for k in reversed(range(FIELDS)):
            v = b[k]
            for j in range(k + 1, FIELDS):
                v -= m[k, j] * delta[j]
            delta[k] = v * inverse[k]
        for k in range(FIELDS):
            lam[k] = jnp.maximum(weights[k] + delta[k], FLOOR * weights[k])

    def newton(it, carry):
        weights = [lam[j] for j in range(FIELDS)]
        main_sums(weights)
        exchange(it, lambda: None)
        solve(weights)
        return carry

    weights = [lam[j] for j in range(FIELDS)]
    main_sums(weights)
    receive(moves_z)
    edge_sums(weights, edge_rows())
    if near:
        pl.semaphore_wait(known, sum(both(o).astype(jnp.int32) for o in plane))
    exchange(0, repair)
    solve(weights)
    lax.fori_loop(1, ITERS, newton, 0)

    weights = [lam[j] for j in range(FIELDS)]
    for k in range(chunks):
        x, t = divmod(k, tiles)
        out_ref[x, t * SUB : (t + 1) * SUB, :] = respond(k, weights)[0]
    final = zero
    for j in range(FIELDS):
        final = jnp.where(lane == j, weights[j], final)
    lam_out[...] = final

    for moves in [moves_c, moves_y] + xs + [moves_z]:
        for send, _, copy in moves:
            pl.when(send)(copy.wait_send)
    for it in range(ITERS):
        for n, axes in enumerate(stages):
            size = math.prod(shape[a] for a in axes)
            whole = recvs[n].at[it, pl.ds(0, size - 1)]
            pltpu.make_async_copy(whole, whole, sum_send.at[it, n]).wait()


def finish(field_ref, lam_ref, field_out, lam_out, row, sem):
    whole = pltpu.make_async_copy(field_ref, field_out, sem.at[0])
    whole.start()
    row[...] = lam_ref[0, :FIELDS]
    short = pltpu.make_async_copy(row, lam_out, sem.at[1])
    short.start()
    whole.wait()
    short.wait()


def shards(shape, density, spread, sensitivities, violation, multipliers_start):
    nx, ny, nz = density.shape
    chunks = nx * ny // SUB
    groups = len(steps())
    stages = plan(shape)
    corners = 9 if shape["gz"] == 2 else 18
    f32 = jnp.float32
    vmem = pl.BlockSpec(memory_space=pltpu.VMEM)
    dma = pltpu.SemaphoreType.DMA
    hbm = pl.BlockSpec(memory_space=pltpu.HBM)
    field, lam = pl.pallas_call(
        functools.partial(body, shape, (nx, ny, nz)),
        out_shape=(
            pltpu.VMEM((nx, ny, nz), f32),
            pltpu.VMEM((SUB, LANE), f32),
        ),
        in_specs=[hbm] * 5,
        out_specs=(vmem, vmem),
        scratch_shapes=[
            pltpu.VMEM((nx, ny, nz), f32),
            pltpu.VMEM((nx, ny, nz), f32),
            pltpu.SMEM((FIELDS,), f32),
            pltpu.SMEM((FIELDS,), f32),
            pltpu.VMEM((FIELDS, nx, ny + 2 * SUB, nz), f32),
            pltpu.VMEM((2, FIELDS, ny + 2 * SUB, nz), f32),
            pltpu.VMEM((2, FIELDS, nx, nz), f32),
            pltpu.VMEM((2, FIELDS, nx, nz), f32),
            pltpu.VMEM((4, FIELDS, 1, nz), f32),
            pltpu.VMEM((4, FIELDS, 1, nz), f32),
            pltpu.VMEM((2, FIELDS, nx, nz), f32),
            pltpu.VMEM((groups, SUB, LANE), f32),
            pltpu.VMEM((2, groups, SUB, LANE), f32),
            pltpu.VMEM((2, SUB, LANE), f32),
            pltpu.VMEM((2, 2, SUB, LANE), f32),
            pltpu.VMEM((2, SUB, LANE), f32),
            pltpu.VMEM((2, 2, SUB, LANE), f32),
            pltpu.VMEM((2, 4, SUB, LANE), f32),
            pltpu.VMEM((3, SUB, LANE), f32),
            pltpu.VMEM((FIELDS, chunks, SUB, LANE), f32),
            pltpu.VMEM((chunks, SUB, LANE), f32),
            pltpu.VMEM((FIELDS + 1, chunks + 1, SUB, LANE), f32),
            pltpu.VMEM((FIELDS + 1, chunks + 1, SUB, LANE), f32),
            pltpu.VMEM((FIELDS, chunks, SUB, LANE), f32),
            pltpu.VMEM((FIELDS, chunks, SUB, LANE), f32),
            pltpu.VMEM((ROWS, SUB, LANE), f32),
            pltpu.VMEM((-(-ROWS // SUB), SUB, LANE), f32),
            pltpu.VMEM((FIELDS, SUB, LANE), f32),
            pltpu.VMEM((ITERS, len(stages), 1, LANE), f32),
        ] + [
            pltpu.VMEM((ITERS, math.prod(shape[a] for a in axes), 1, LANE), f32) for axes in stages
        ] + [
            dma((5,)), dma((6 + 2 * groups,)), dma((6 + 2 * groups,)), dma((corners,)), dma((corners,)),
            dma((ITERS, len(stages))), dma((ITERS, len(stages))), pltpu.SemaphoreType.REGULAR,
        ],
        compiler_params=pltpu.CompilerParams(
            collective_id=0, has_side_effects=True, vmem_limit_bytes=24 << 20),
        name="design_step",
    )(*[pltpu.with_memory_space_constraint(v, pltpu.HBM) for v in (density, spread, sensitivities, violation, multipliers_start)])
    return pl.pallas_call(
        finish,
        out_shape=(
            jax.ShapeDtypeStruct((nx, ny, nz), f32),
            jax.ShapeDtypeStruct((FIELDS,), f32),
        ),
        in_specs=[vmem, vmem],
        out_specs=(hbm, hbm),
        scratch_shapes=[pltpu.VMEM((FIELDS,), f32), dma((2,))],
        compiler_params=pltpu.CompilerParams(vmem_limit_bytes=1 << 20),
        name="finish",
    )(field, lam)


def solution(mesh):
    shape = {a: int(mesh.shape[a]) for a in AXES}
    return jax.shard_map(
        functools.partial(shards, shape),
        mesh=mesh,
        in_specs=(P("gx", "gy", "gz"), P("gx", "gy", "gz"), P(None, "gx", "gy", "gz"), P(), P()),
        out_specs=(P("gx", "gy", "gz"), P()),
        check_vma=False,
    )
```

time: 29.9 us -> 28.1 us (0.940)
  Pallas kernels: 29.2 us -> 27.3 us
    pallas_call x1, Pallas kernels: 28.5 us -> 26.7 us  [shards(): pl.pallas_call(functools.partial(body, shape, (nx, ny, nz)), out_shape=(p...]
where the time goes in v2:
time: 28.1 us; the launch traced here: 28 us
  Pallas kernels  27.3 us (97%)
  between operations  0.64 us (2%)
    pallas_call x1, Pallas kernels, shards(): pl.pallas_call(functools.partial(body, shape, (nx, ny, nz)), out_shape=(p...  26.7 us
    pallas_call x1, Pallas kernels, shards(): pl.pallas_call(finish, out_shape=(jax.ShapeDtypeStruct((nx, ny, nz), f32)...  0.65 us

profile of v2, /device:TPU:0, one launch (start us, length us, event | category | flops | bytes accessed | tf_op | source)
XLA Modules:
  0.0 28.0 jit_solution(4167234971606055714)
XLA Ops:
  0.6 26.7 %design_step.1 = (f32[8,16,128]{2,1,0:T(8,128)S(1)}, f32[8,128]{1,0:T(8,128)S(1)}) custom-call(f32[8,16,128]{2,1,0:T(8,128)} %dens_hbm.1, f32[8,16,128]{2,1,0:T(8,128)} %span_hbm.1, f32[9,8,16,128]{3,2,1,0:T(8,128)} %sens_ref.1, f32[9]{0:T(128)} %viol_hbm.1, f32[9]{0:T(128)} %lam0_hbm.1), custom_call_target="tpu_custom_call" | custom-call | tf_op jit(solution)/shard_map/design_step/pallas_call | solution.py:613
  27.3 0.7 %finish.1 = (f32[8,16,128]{2,1,0:T(8,128)}, f32[9]{0:T(128)}) custom-call(f32[8,16,128]{2,1,0:T(8,128)S(1)} %get-tuple-element.4.field_ref, f32[8,128]{1,0:T(8,128)S(1)} %get-tuple-element.5.lam_ref), custom_call_target="tpu_custom_call" | custom-call | tf_op jit(solution)/shard_map/finish/pallas_call | solution.py:661

commit v3 on v2

--- a/solution.py
+++ b/solution.py
@@ -49,7 +49,7 @@
 
 
 def body(shape, dims, dens_hbm, span_hbm, sens_ref, viol_hbm, lam0_hbm, out_ref, lam_out,
-         dens_ref, span_ref, viol_ref, lam0_ref, pad, xpad, ypack, yrecv, cpack, crecv, ycorr,
+         dens_ref, span_ref, viol_ref, lam0_ref, pad, xpad, ypack, yrecv, cpack, crecv, ymid,
          zpack, zrecv, xzpack, xzrecv, yzpack, yzrecv, czrecv, around, mid, invden, pp, qq, slope, scaled,
          acc, wide, lam, part, *rest):
     stages = plan(shape)
@@ -59,6 +59,17 @@
     tiles = ny // SUB
     chunks = nx * tiles
     slots = 2 * chunks
+    load = pltpu.make_async_copy(
+        sens_ref, pad.at[:, :, SUB : SUB + ny, :], load_sem.at[0]
+    )
+    load.start()
+    small = [
+        pltpu.make_async_copy(src, dst, load_sem.at[1 + i])
+        for i, (src, dst) in enumerate([
+            (span_hbm, span_ref), (dens_hbm, dens_ref), (viol_hbm, viol_ref), (lam0_hbm, lam0_ref)])
+    ]
+    for copy in small:
+        copy.start()
     wide_x = 2 * tiles
     groups = steps()
     count_of = len(groups)
@@ -103,18 +114,6 @@
             target = {a: lax.rem(me[a] + d, shape[a]) for a, d in zip(AXES, o)}
             pl.semaphore_signal(barrier, inc=1, device_id=target, device_id_type=MESH)
         arrivals = len(partners)
-
-    load = pltpu.make_async_copy(
-        sens_ref, pad.at[:, :, SUB : SUB + ny, :], load_sem.at[0]
-    )
-    load.start()
-    small = [
-        pltpu.make_async_copy(src, dst, load_sem.at[1 + i])
-        for i, (src, dst) in enumerate([
-            (span_hbm, span_ref), (dens_hbm, dens_ref), (viol_hbm, viol_ref), (lam0_hbm, lam0_ref)])
-    ]
-    for copy in small:
-        copy.start()
 
     lane = lax.broadcasted_iota(jnp.int32, (SUB, LANE), 1)
     row = lax.broadcasted_iota(jnp.int32, (SUB, LANE), 0)
@@ -258,6 +257,15 @@
         for _, expected, copy in moves:
             pl.when(expected)(copy.wait_recv)
 
+    friends = sum(both(o).astype(jnp.int32) for o in plane)
+
+    def tell(n):
+        for o in plane:
+            @pl.when(both(o))
+            def _(o=o):
+                pl.semaphore_signal(known.at[n], inc=1, device_id=at(gy=o[1], gx=o[2]),
+                                    device_id_type=MESH)
+
     xs = [moves_x(g) for g in range(count_of)]
     start(moves_z)
     start(moves_c)
@@ -265,6 +273,8 @@
     start(moves_y)
     for g in range(1, count_of):
         start(xs[g])
+    if near:
+        tell(0)
 
     def along(s0, s1):
         up = jnp.where(lane == 0, 0.0, pltpu.roll(s1, 1, 1))
@@ -301,7 +311,12 @@
             value = ref[k] if n == 2 else piece(ref, k)
             for j in range(LANE // slots):
                 packed = place(packed, value, k, j)
-        around[n] = packed
+        around[n, 0] = packed
+        for i, y in enumerate((0, ny - 1)):
+            for x in range(nx):
+                k = x * tiles + y // SUB
+                around[n, 1 + i, x : x + 1, :] = (
+                    ref[k, y % SUB : y % SUB + 1, :] if n == 2 else ref[x, y : y + 1, :])
     for k in range(FIELDS):
         lam[k] = jnp.full((SUB, LANE), lam0_ref[k], jnp.float32)
     total = zero
@@ -312,22 +327,17 @@
         qq[FIELDS, k] = square * (0.001 + RAA)
         total += s * (1.002 + 2 * RAA)
     acc[ROWS - 1] = total
-
-    receive(moves_c)
-    receive(moves_y)
-    x_row = lax.broadcasted_iota(jnp.int32, (nx, LANE), 0)
-    x_lane = lax.broadcasted_iota(jnp.int32, (nx, LANE), 1)
-    for i in range(2):
-        for f in range(FIELDS):
-            h = yrecv[i, f]
-            low = jnp.broadcast_to(crecv[i, f], (nx, LANE))
-            high = jnp.broadcast_to(crecv[2 + i, f], (nx, LANE))
-            pair = jnp.where(x_row == 0, low, pltpu.roll(h, 1, 0)) + jnp.where(x_row == nx - 1, high, pltpu.roll(h, nx - 1, 0))
-            s0 = W1 * h + W2 * pair
-            s1 = W2 * h + W3 * pair
-            up = jnp.where(x_lane == 0, 0.0, pltpu.roll(s1, 1, 1))
-            down = jnp.where(x_lane == LANE - 1, 0.0, pltpu.roll(s1, LANE - 1, 1))
-            ycorr[i, f] = s0 + up + down
+    weights = [lam[j] for j in range(FIELDS)]
+
+    inside = jnp.logical_not(ends)
+
+    def keep_of(k):
+        keep = inside
+        if k % tiles == 0:
+            keep = jnp.logical_and(keep, row != 0)
+        if k % tiles == tiles - 1:
+            keep = jnp.logical_and(keep, row != SUB - 1)
+        return keep
 
     def grown(r, s):
         gp = jnp.maximum(r, 0.0)
@@ -337,49 +347,35 @@
         q = square * (0.001 * gp + 1.001 * gm + RAA)
         return p, q, s * (1.002 * (gp + gm) + 2 * RAA)
 
-    def rows(f, j, packed):
+    def rows(f, j, packed, ks):
         total = zero
-        for k in range(chunks):
+        for k in ks:
             x, t = divmod(k, tiles)
             value = mid[f, k]
-            if t == 0:
-                value += jnp.where(row == 0, jnp.broadcast_to(ycorr[0, f, x : x + 1, :], (SUB, LANE)), 0.0)
-            if t == tiles - 1:
-                value += jnp.where(row == SUB - 1, jnp.broadcast_to(ycorr[1, f, x : x + 1, :], (SUB, LANE)), 0.0)
             for i in range(2):
                 if x == (0, nx - 1)[i]:
                     y = SUB + t * SUB
                     h = xpad[i, f, y : y + SUB, :]
                     pair = xpad[i, f, y - 1 : y - 1 + SUB, :] + xpad[i, f, y + 1 : y + 1 + SUB, :]
                     value += along(W1 * h + W2 * pair, W2 * h + W3 * pair)
+            for i, y in enumerate((0, ny - 1)):
+                if t == y // SUB:
+                    ymid[i, f, x : x + 1, :] = value[y % SUB : y % SUB + 1, :]
             packed = place(packed, value, k, j)
-            pp[f, k], qq[f, k], base = grown(value * invden[k], piece(span_ref, k))
-            total += base
+            s = piece(span_ref, k)
+            pp[f, k], qq[f, k], base = grown(value * invden[k], s)
+            total += jnp.where(keep_of(k), base, 0.0)
         if f:
-            acc[SUMS - 1 + f] = total
+            acc[SUMS - 1 + f] = total + (zero if ks is core else acc[SUMS - 1 + f])
         return packed
-
-    inner = []
-    for g, fields in enumerate(groups):
-        receive(xs[g])
-        if near and g == 0:
-            for o in plane:
-                @pl.when(both(o))
-                def _(o=o):
-                    pl.semaphore_signal(known, inc=1, device_id=at(gy=o[1], gx=o[2]),
-                                        device_id_type=MESH)
-        packed = zero
-        for j, f in enumerate(fields):
-            packed = rows(f, j, packed)
-        inner.append(packed)
 
     def respond(k, weights):
         big_p, big_q = pp[0, k], qq[0, k]
         for j in range(FIELDS):
             big_p += weights[j] * pp[j + 1, k]
             big_q += weights[j] * qq[j + 1, k]
-        s = around[0] if k == chunks else piece(span_ref, k)
-        d = around[1] if k == chunks else piece(dens_ref, k)
+        s = piece(span_ref, k) if k < chunks else around[0, k - chunks]
+        d = piece(dens_ref, k) if k < chunks else around[1, k - chunks]
         root_p = jnp.sqrt(big_p)
         root_q = jnp.sqrt(big_q)
         lower, upper = d - s, d + s
@@ -388,12 +384,14 @@
         high = jnp.minimum(1.0, d + MOVE * s)
         return jnp.minimum(jnp.maximum(moved, low), high), big_p, big_q, lower, upper
 
-    def terms(k, weights):
+    def terms(k, weights, keep=None):
         moved, big_p, big_q, lower, upper = respond(k, weights)
         ia = 1.0 / (upper - moved)
         ib = 1.0 / (moved - lower)
         ia2, ib2 = ia * ia, ib * ib
         inv = 1.0 / (2.0 * big_p * (ia2 * ia) + 2.0 * big_q * (ib2 * ib))
+        if keep is not None:
+            ia, ib, ia2, ib2 = [jnp.where(keep, v, 0.0) for v in (ia, ib, ia2, ib2)]
         grads, slopes, ratios = [], [], []
         for j in range(FIELDS):
             p, q = pp[j + 1, k], qq[j + 1, k]
@@ -403,26 +401,27 @@
             ratios.append(a * inv)
         return grads, slopes, ratios
 
-    def main_sums(weights):
-        grads = [zero] * FIELDS
-        for k in range(chunks):
-            more, slopes, ratios = terms(k, weights)
+    def main_sums(weights, ks, masked, more):
+        grads = [acc[j] if more else zero for j in range(FIELDS)]
+        for k in ks:
+            extra, slopes, ratios = terms(k, weights, keep_of(k) if masked else None)
             for j in range(FIELDS):
-                grads[j] += more[j]
+                grads[j] += extra[j]
                 slope[j, k] = slopes[j]
                 scaled[j, k] = ratios[j]
         for j in range(FIELDS):
             acc[j] = grads[j]
         at_row = FIELDS
         for group in ((0, 1), (2, 3), (4, 5, 6, 7, 8)):
-            sums = {(i, j): zero for i in group for j in range(i, FIELDS)}
-            for k in range(chunks):
+            keys = [(i, j) for i in group for j in range(i, FIELDS)]
+            sums = {key: acc[at_row + n] if more else zero for n, key in enumerate(keys)}
+            for k in ks:
                 right = {j: slope[j, k] for j in range(group[0], FIELDS)}
                 for i in group:
                     left = scaled[i, k]
                     for j in range(i, FIELDS):
                         sums[i, j] += left * right[j]
-            for key in sums:
+            for key in keys:
                 acc[at_row] = sums[key]
                 at_row += 1
 
@@ -460,32 +459,77 @@
             out.append(W1 * c + W2 * (s + pair(c, c_low, c_high)) + W3 * pair(s, s_low, s_high))
         return out
 
-    def edge_rows():
-        outer = outer_edges()
-        s = around[0]
+    def face_rows():
+        drops = [[zero, zero] for _ in groups]
         bases = []
         for g, fields in enumerate(groups):
-            p, q, base = grown((inner[g] + outer[g]) * around[2], s)
+            for j, f in enumerate(fields):
+                base = zero
+                for i in range(2):
+                    h = yrecv[i, f]
+                    low = jnp.broadcast_to(crecv[i, f], (SUB, LANE))
+                    high = jnp.broadcast_to(crecv[2 + i, f], (SUB, LANE))
+                    pair = (jnp.where(row == 0, low, pltpu.roll(h, 1, 0))
+                            + jnp.where(row == nx - 1, high, pltpu.roll(h, nx - 1, 0)))
+                    extra = along(W1 * h + W2 * pair, W2 * h + W3 * pair)
+                    s = around[0, 1 + i]
+                    p, q, more = grown((ymid[i, f] + extra) * around[2, 1 + i], s)
+                    pp[f, chunks + 1 + i] = p
+                    qq[f, chunks + 1 + i] = q
+                    base += jnp.where(inside, more, 0.0)
+                    here = jnp.logical_and(row == x_of, lane // slots == j)
+                    side = jnp.where(odd, jnp.broadcast_to(extra[:, :1], (SUB, LANE)),
+                                     jnp.broadcast_to(extra[:, LANE - 1 :], (SUB, LANE)))
+                    drops[g][i] = jnp.where(here, side, drops[g][i])
+                bases.append(base)
+        for i in range(2):
+            s = around[0, 1 + i]
+            pp[FIELDS, chunks + 1 + i] = s * s * (1.001 + RAA)
+            qq[FIELDS, chunks + 1 + i] = s * s * (0.001 + RAA)
+        extras = []
+        for g in range(count_of):
+            value = zero
+            for i, y in enumerate((0, ny - 1)):
+                full = jnp.broadcast_to(jnp.sum(drops[g][i], axis=0, keepdims=True), (SUB, LANE))
+                here = jnp.logical_and(row == y % SUB, t_of == y // SUB)
+                value += jnp.where(here, full, 0.0)
+            extras.append(value)
+        return extras, bases[1:]
+
+    def edge_rows(extras):
+        outer = outer_edges()
+        s = around[0, 0]
+        bases = []
+        for g, fields in enumerate(groups):
+            p, q, base = grown((inner[g] + extras[g] + outer[g]) * around[2, 0], s)
             for j, f in enumerate(fields):
                 pp[f, chunks] = turned(p, -j * slots)
                 qq[f, chunks] = turned(q, -j * slots)
                 bases.append(turned(base, -j * slots))
         pp[FIELDS, chunks] = s * s * (1.001 + RAA)
         qq[FIELDS, chunks] = s * s * (0.001 + RAA)
-        return bases[1:] + [s * (1.002 + 2 * RAA)]
-
-    def edge_sums(weights, bases):
-        grads, slopes, ratios = terms(chunks, weights)
-        more = grads + [ratios[i] * slopes[j] for i in range(FIELDS) for j in range(i, FIELDS)] + bases
-        for r in range(ROWS):
-            acc[r] = jnp.where(ends, 0.0, acc[r]) + jnp.where(lane < slots, more[r], 0.0)
+        return bases[1:]
+
+    def extra_sums(weights, ks, keep, bases):
+        pieces = [terms(k, weights, keep) for k in ks]
+        grads = [sum((p[0][j] for p in pieces[1:]), pieces[0][0][j]) for j in range(FIELDS)]
+        squares = [sum((p[2][i] * p[1][j] for p in pieces[1:]), pieces[0][2][i] * pieces[0][1][j])
+                   for i in range(FIELDS) for j in range(i, FIELDS)]
+        for r, value in enumerate(grads + squares + list(bases)):
+            acc[r] += value
 
     def repair():
         for f in range(FIELDS):
-            p, q = pp[f, chunks], qq[f, chunks]
-            for k in range(chunks):
-                pp[f, k] = jnp.where(ends, turned(p, -2 * k - 1), pp[f, k])
-                qq[f, k] = jnp.where(ends, turned(q, -2 * k - 1), qq[f, k])
+            for ref in (pp, qq):
+                edge = ref[f, chunks]
+                for k in range(chunks):
+                    x, t = divmod(k, tiles)
+                    value = ref[f, k]
+                    for i, y in enumerate((0, ny - 1)):
+                        if t == y // SUB:
+                            line = jnp.broadcast_to(ref[f, chunks + 1 + i, x : x + 1, :], (SUB, LANE))
+                            value = jnp.where(row == y % SUB, line, value)
+                    ref[f, k] = jnp.where(ends, turned(edge, -2 * k - 1), value)
 
     def flat(axes):
         index = 0
@@ -556,17 +600,38 @@
 
     def newton(it, carry):
         weights = [lam[j] for j in range(FIELDS)]
-        main_sums(weights)
+        main_sums(weights, range(chunks), False, False)
         exchange(it, lambda: None)
         solve(weights)
         return carry
 
-    weights = [lam[j] for j in range(FIELDS)]
-    main_sums(weights)
+    core = range(tiles, chunks - tiles)
+    faces = [k for k in range(chunks) if k not in core]
+    inner = []
+    for g, fields in enumerate(groups):
+        packed = zero
+        for j, f in enumerate(fields):
+            packed = rows(f, j, packed, core)
+        inner.append(packed)
+    main_sums(weights, core, True, False)
+    if near:
+        pl.semaphore_wait(known.at[0], friends)
+        tell(1)
+    receive(moves_y)
+    for g, fields in enumerate(groups):
+        receive(xs[g])
+        for j, f in enumerate(fields):
+            inner[g] = rows(f, j, inner[g], faces)
+    main_sums(weights, faces, True, True)
+    receive(moves_c)
+    extras, bases = face_rows()
+    extra_sums(weights, (chunks + 1, chunks + 2), inside, bases)
     receive(moves_z)
-    edge_sums(weights, edge_rows())
+    within = lane < slots
+    bases = [jnp.where(within, v, 0.0) for v in edge_rows(extras)]
+    extra_sums(weights, (chunks,), within, bases)
     if near:
-        pl.semaphore_wait(known, sum(both(o).astype(jnp.int32) for o in plane))
+        pl.semaphore_wait(known.at[1], friends)
     exchange(0, repair)
     solve(weights)
     lax.fori_loop(1, ITERS, newton, 0)
@@ -637,11 +702,11 @@
             pltpu.VMEM((2, SUB, LANE), f32),
             pltpu.VMEM((2, 2, SUB, LANE), f32),
             pltpu.VMEM((2, 4, SUB, LANE), f32),
-            pltpu.VMEM((3, SUB, LANE), f32),
+            pltpu.VMEM((3, 3, SUB, LANE), f32),
             pltpu.VMEM((FIELDS, chunks, SUB, LANE), f32),
             pltpu.VMEM((chunks, SUB, LANE), f32),
-            pltpu.VMEM((FIELDS + 1, chunks + 1, SUB, LANE), f32),
-            pltpu.VMEM((FIELDS + 1, chunks + 1, SUB, LANE), f32),
+            pltpu.VMEM((FIELDS + 1, chunks + 3, SUB, LANE), f32),
+            pltpu.VMEM((FIELDS + 1, chunks + 3, SUB, LANE), f32),
             pltpu.VMEM((FIELDS, chunks, SUB, LANE), f32),
             pltpu.VMEM((FIELDS, chunks, SUB, LANE), f32),
             pltpu.VMEM((ROWS, SUB, LANE), f32),
@@ -652,7 +717,7 @@
             pltpu.VMEM((ITERS, math.prod(shape[a] for a in axes), 1, LANE), f32) for axes in stages
         ] + [
             dma((5,)), dma((6 + 2 * groups,)), dma((6 + 2 * groups,)), dma((corners,)), dma((corners,)),
-            dma((ITERS, len(stages))), dma((ITERS, len(stages))), pltpu.SemaphoreType.REGULAR,
+            dma((ITERS, len(stages))), dma((ITERS, len(stages))), pltpu.SemaphoreType.REGULAR((2,)),
         ],
         compiler_params=pltpu.CompilerParams(
             collective_id=0, has_side_effects=True, vmem_limit_bytes=24 << 20),

time: 28.1 us -> 27.8 us (0.989)
  Pallas kernels: 27.3 us -> 27 us
    pallas_call x1, Pallas kernels: 26.7 us -> 26.4 us  [shards(): pl.pallas_call(functools.partial(body, shape, (nx, ny, nz)), out_shape=(p...]
where the time goes in v3:
time: 27.8 us; the launch traced here: 27.7 us
  Pallas kernels  27 us (97%)
  between operations  0.64 us (2%)
    pallas_call x1, Pallas kernels, shards(): pl.pallas_call(functools.partial(body, shape, (nx, ny, nz)), out_shape=(p...  26.4 us
    pallas_call x1, Pallas kernels, shards(): pl.pallas_call(finish, out_shape=(jax.ShapeDtypeStruct((nx, ny, nz), f32)...  0.65 us

profile of v3, /device:TPU:0, one launch (start us, length us, event | category | flops | bytes accessed | tf_op | source)
XLA Modules:
  0.0 27.7 jit_solution(1301955412573064370)
XLA Ops:
  0.6 26.4 %design_step.1 = (f32[8,16,128]{2,1,0:T(8,128)S(1)}, f32[8,128]{1,0:T(8,128)S(1)}) custom-call(f32[8,16,128]{2,1,0:T(8,128)} %dens_hbm.1, f32[8,16,128]{2,1,0:T(8,128)} %span_hbm.1, f32[9,8,16,128]{3,2,1,0:T(8,128)} %sens_ref.1, f32[9]{0:T(128)} %viol_hbm.1, f32[9]{0:T(128)} %lam0_hbm.1), custom_call_target="tpu_custom_call" | custom-call | tf_op jit(solution)/shard_map/design_step/pallas_call | solution.py:678
  27.0 0.7 %finish.1 = (f32[8,16,128]{2,1,0:T(8,128)}, f32[9]{0:T(128)}) custom-call(f32[8,16,128]{2,1,0:T(8,128)S(1)} %get-tuple-element.4.field_ref, f32[8,128]{1,0:T(8,128)S(1)} %get-tuple-element.5.lam_ref), custom_call_target="tpu_custom_call" | custom-call | tf_op jit(solution)/shard_map/finish/pallas_call | solution.py:726

commit v4 on v3

--- a/solution.py
+++ b/solution.py
@@ -82,15 +82,26 @@
         has[a, 1] = me[a] < shape[a] - 1
 
     def both(o):
-        moved = [has[a, d] for a, d in zip(AXES, o) if d]
-        return functools.reduce(jnp.logical_and, moved)
+        moved = [has[a, d] for a, d in zip(AXES, o) if d and not (single and a == "gz")]
+        return functools.reduce(jnp.logical_and, moved, jnp.bool_(True))
+
+    single = shape["gz"] == 2
+    if single:
+        has["gz", 1] = jnp.bool_(True)
 
     def at(**moves):
-        return {a: me[a] + d for a, d in moves.items()}
+        out = {a: me[a] + d for a, d in moves.items()}
+        if single and moves.get("gz"):
+            out["gz"] = 1 - me["gz"]
+        return out
 
     signs = (-1, 0, 1)
     plane = [(0, dy, dx) for dy in signs for dx in signs if dy or dx]
-    ring = [(dz, dy, dx) for dz in signs for dy in signs for dx in signs if dz or dy or dx]
+    ring = [(dz, dy, dx) for dz in ((1, 0) if single else signs) for dy in signs for dx in signs if dz or dy or dx]
+    ring.sort(key=lambda o: (-sum(map(abs, o)), o))
+    if single:
+        has["gz", -1] = has["gz", 1]
+    sides = ((0, 1),) if single else ((0, 1), (1, -1))
     barrier = pltpu.get_barrier_semaphore()
     near = shape["gz"] == 2 and shape["gy"] <= 4 and shape["gx"] <= 4
     if near:
@@ -145,16 +156,17 @@
         @pl.when(jnp.logical_not(jnp.logical_and(has["gx", -sx], has["gy", -sy])))
         def _(i=i):
             crecv[i] = jnp.zeros((FIELDS, 1, LANE), jnp.float32)
-    for i, sz in enumerate((1, -1)):
-        @pl.when(jnp.logical_not(has["gz", -sz]))
-        def _(i=i):
-            zrecv[i] = jnp.zeros(zrecv.shape[1:], jnp.float32)
+    for i, sz in sides:
+        if not single:
+            @pl.when(jnp.logical_not(has["gz", -sz]))
+            def _(i=i):
+                zrecv[i] = jnp.zeros(zrecv.shape[1:], jnp.float32)
         for n, sx in enumerate((1, -1)):
-            @pl.when(jnp.logical_not(jnp.logical_and(has["gz", -sz], has["gx", -sx])))
+            @pl.when(jnp.logical_not(both((-sz, 0, -sx))))
             def _(i=i, n=n):
                 xzrecv[i, n] = zero
         for n, sy in enumerate((1, -1)):
-            @pl.when(jnp.logical_not(jnp.logical_and(has["gz", -sz], has["gy", -sy])))
+            @pl.when(jnp.logical_not(both((-sz, -sy, 0))))
             def _(i=i, n=n):
                 yzrecv[i, n] = zero
         for n, (sx, sy) in enumerate(corners):
@@ -219,8 +231,8 @@
         copy = pltpu.make_async_remote_copy(
             src_ref=src, dst_ref=dst, send_sem=sends.at[index], recv_sem=recvs_.at[index],
             device_id=at(**moves), device_id_type=MESH)
-        there = functools.reduce(jnp.logical_and, [has[a, d] for a, d in moves.items()])
-        back = functools.reduce(jnp.logical_and, [has[a, -d] for a, d in moves.items()])
+        there = both([moves.get(a, 0) for a in AXES])
+        back = both([-moves.get(a, 0) for a in AXES])
         return there, back, copy
 
     def moves_x(g):
@@ -236,8 +248,8 @@
     moves_y = [remote(ypack.at[i], yrecv.at[i], send_sem, recv_sem, i, gy=sy)
                for i, sy in enumerate((1, -1))]
     moves_z = []
-    for i, sz in enumerate((1, -1)):
-        first = 0 if shape["gz"] == 2 else 9 * i
+    for i, sz in sides:
+        first = 9 * i
         for n, (sx, sy) in enumerate(corners):
             moves_z.append(remote(yzpack.at[n % 2], czrecv.at[i, n], zsend_sem, zrecv_sem, first + 5 + n,
                                   gz=sz, gx=sx, gy=sy))
@@ -330,9 +342,13 @@
     weights = [lam[j] for j in range(FIELDS)]
 
     inside = jnp.logical_not(ends)
+    core = range(tiles, chunks - tiles)
+    faces = [k for k in range(chunks) if k not in core]
 
     def keep_of(k):
         keep = inside
+        if k in faces:
+            return keep
         if k % tiles == 0:
             keep = jnp.logical_and(keep, row != 0)
         if k % tiles == tiles - 1:
@@ -358,10 +374,14 @@
                     h = xpad[i, f, y : y + SUB, :]
                     pair = xpad[i, f, y - 1 : y - 1 + SUB, :] + xpad[i, f, y + 1 : y + 1 + SUB, :]
                     value += along(W1 * h + W2 * pair, W2 * h + W3 * pair)
+            packed = place(packed, value, k, j)
             for i, y in enumerate((0, ny - 1)):
                 if t == y // SUB:
-                    ymid[i, f, x : x + 1, :] = value[y % SUB : y % SUB + 1, :]
-            packed = place(packed, value, k, j)
+                    if k in faces:
+                        line = jnp.broadcast_to(ymid[i, f, x : x + 1, :], (SUB, LANE))
+                        value += jnp.where(row == y % SUB, line, 0.0)
+                    else:
+                        ymid[i, f, x : x + 1, :] = value[y % SUB : y % SUB + 1, :]
             s = piece(span_ref, k)
             pp[f, k], qq[f, k], base = grown(value * invden[k], s)
             total += jnp.where(keep_of(k), base, 0.0)
@@ -426,7 +446,13 @@
                 at_row += 1
 
     def combined(ref, *index):
-        return jnp.where(odd, pltpu.roll(ref[(0,) + index], 1, 1), pltpu.roll(ref[(1,) + index], LANE - 1, 1))
+        last = 0 if single else 1
+        low = pltpu.roll(ref[(0,) + index], 1, 1)
+        high = pltpu.roll(ref[(last,) + index], LANE - 1, 1)
+        if single:
+            upper = me["gz"] == 1
+            return jnp.where(odd, jnp.where(upper, low, 0.0), jnp.where(upper, 0.0, high))
+        return jnp.where(odd, low, high)
 
     def outer_edges():
         last_x, last_t = wide_x * (nx - 1), 2 * (tiles - 1)
@@ -458,6 +484,8 @@
                         + jnp.where(x_of == nx - 1, high, turned(own, -wide_x)))
             out.append(W1 * c + W2 * (s + pair(c, c_low, c_high)) + W3 * pair(s, s_low, s_high))
         return out
+
+    body_rows = jnp.logical_and(inside, jnp.logical_and(row != 0, row != nx - 1))
 
     def face_rows():
         drops = [[zero, zero] for _ in groups]
@@ -473,10 +501,14 @@
                             + jnp.where(row == nx - 1, high, pltpu.roll(h, nx - 1, 0)))
                     extra = along(W1 * h + W2 * pair, W2 * h + W3 * pair)
                     s = around[0, 1 + i]
-                    p, q, more = grown((ymid[i, f] + extra) * around[2, 1 + i], s)
+                    face = jnp.logical_or(row == 0, row == nx - 1)
+                    value = jnp.where(face, 0.0, ymid[i, f]) + extra
+                    p, q, more = grown(value * around[2, 1 + i], s)
                     pp[f, chunks + 1 + i] = p
                     qq[f, chunks + 1 + i] = q
-                    base += jnp.where(inside, more, 0.0)
+                    base += jnp.where(body_rows, more, 0.0)
+                    ymid[i, f, 0:1, :] = extra[:1]
+                    ymid[i, f, nx - 1 : nx, :] = extra[nx - 1 :]
                     here = jnp.logical_and(row == x_of, lane // slots == j)
                     side = jnp.where(odd, jnp.broadcast_to(extra[:, :1], (SUB, LANE)),
                                      jnp.broadcast_to(extra[:, LANE - 1 :], (SUB, LANE)))
@@ -518,6 +550,12 @@
         for r, value in enumerate(grads + squares + list(bases)):
             acc[r] += value
 
+    def between():
+        repair()
+        for moves in [moves_c, moves_y] + xs + [moves_z]:
+            for send, _, copy in moves:
+                pl.when(send)(copy.wait_send)
+
     def repair():
         for f in range(FIELDS):
             for ref in (pp, qq):
@@ -526,7 +564,7 @@
                     x, t = divmod(k, tiles)
                     value = ref[f, k]
                     for i, y in enumerate((0, ny - 1)):
-                        if t == y // SUB:
+                        if t == y // SUB and k in core:
                             line = jnp.broadcast_to(ref[f, chunks + 1 + i, x : x + 1, :], (SUB, LANE))
                             value = jnp.where(row == y % SUB, line, value)
                     ref[f, k] = jnp.where(ends, turned(edge, -2 * k - 1), value)
@@ -539,8 +577,20 @@
 
     def exchange(it, meanwhile):
         packed = zero
-        for r in range(ROWS):
-            packed = jnp.where(lane == r, jnp.sum(acc[r], axis=1, keepdims=True), packed)
+        for g in range(wide.shape[0]):
+            values = [acc[r] if r < ROWS else zero for r in range(g * SUB, (g + 1) * SUB)]
+            half = SUB // 2
+            while half:
+                upper = (row // half) % 2 == 1
+                step = len(values) // 2
+                values = [
+                    jnp.where(upper, b, a) + pltpu.roll(jnp.where(upper, a, b), half, 0)
+                    if half == SUB // 2 else
+                    jnp.where(upper, b + turned(b, half, 0), a + turned(a, -half, 0))
+                    for a, b in zip(values[:step], values[step:])
+                ]
+                half //= 2
+            packed = jnp.where(lane == g * SUB + row, jnp.sum(values[0], axis=1, keepdims=True), packed)
         value = jnp.sum(packed, axis=0, keepdims=True)
         for n, axes in enumerate(stages):
             size = math.prod(shape[a] for a in axes)
@@ -605,8 +655,6 @@
         solve(weights)
         return carry
 
-    core = range(tiles, chunks - tiles)
-    faces = [k for k in range(chunks) if k not in core]
     inner = []
     for g, fields in enumerate(groups):
         packed = zero
@@ -618,21 +666,21 @@
         pl.semaphore_wait(known.at[0], friends)
         tell(1)
     receive(moves_y)
+    receive(moves_c)
+    extras, bases = face_rows()
+    extra_sums(weights, (chunks + 1, chunks + 2), body_rows, bases)
     for g, fields in enumerate(groups):
         receive(xs[g])
         for j, f in enumerate(fields):
             inner[g] = rows(f, j, inner[g], faces)
     main_sums(weights, faces, True, True)
-    receive(moves_c)
-    extras, bases = face_rows()
-    extra_sums(weights, (chunks + 1, chunks + 2), inside, bases)
     receive(moves_z)
     within = lane < slots
     bases = [jnp.where(within, v, 0.0) for v in edge_rows(extras)]
     extra_sums(weights, (chunks,), within, bases)
     if near:
         pl.semaphore_wait(known.at[1], friends)
-    exchange(0, repair)
+    exchange(0, between)
     solve(weights)
     lax.fori_loop(1, ITERS, newton, 0)
 
@@ -645,9 +693,6 @@
         final = jnp.where(lane == j, weights[j], final)
     lam_out[...] = final
 
-    for moves in [moves_c, moves_y] + xs + [moves_z]:
-        for send, _, copy in moves:
-            pl.when(send)(copy.wait_send)
     for it in range(ITERS):
         for n, axes in enumerate(stages):
             size = math.prod(shape[a] for a in axes)
@@ -671,6 +716,7 @@
     groups = len(steps())
     stages = plan(shape)
     corners = 9 if shape["gz"] == 2 else 18
+    depth = corners // 9
     f32 = jnp.float32
     vmem = pl.BlockSpec(memory_space=pltpu.VMEM)
     dma = pltpu.SemaphoreType.DMA
@@ -696,12 +742,12 @@
             pltpu.VMEM((4, FIELDS, 1, nz), f32),
             pltpu.VMEM((2, FIELDS, nx, nz), f32),
             pltpu.VMEM((groups, SUB, LANE), f32),
-            pltpu.VMEM((2, groups, SUB, LANE), f32),
+            pltpu.VMEM((depth, groups, SUB, LANE), f32),
             pltpu.VMEM((2, SUB, LANE), f32),
-            pltpu.VMEM((2, 2, SUB, LANE), f32),
+            pltpu.VMEM((depth, 2, SUB, LANE), f32),
             pltpu.VMEM((2, SUB, LANE), f32),
-            pltpu.VMEM((2, 2, SUB, LANE), f32),
-            pltpu.VMEM((2, 4, SUB, LANE), f32),
+            pltpu.VMEM((depth, 2, SUB, LANE), f32),
+            pltpu.VMEM((depth, 4, SUB, LANE), f32),
             pltpu.VMEM((3, 3, SUB, LANE), f32),
             pltpu.VMEM((FIELDS, chunks, SUB, LANE), f32),
             pltpu.VMEM((chunks, SUB, LANE), f32),

time: 27.8 us -> 27.4 us (0.986)
  Pallas kernels: 27 us -> 26.6 us
    pallas_call x1, Pallas kernels: 26.4 us -> 25.9 us  [shards(): pl.pallas_call(functools.partial(body, shape, (nx, ny, nz)), out_shape=(p...]
where the time goes in v4:
time: 27.4 us; the launch traced here: 27.2 us
  Pallas kernels  26.6 us (97%)
  between operations  0.64 us (2%)
    pallas_call x1, Pallas kernels, shards(): pl.pallas_call(functools.partial(body, shape, (nx, ny, nz)), out_shape=(p...  25.9 us
    pallas_call x1, Pallas kernels, shards(): pl.pallas_call(finish, out_shape=(jax.ShapeDtypeStruct((nx, ny, nz), f32)...  0.65 us

profile of v4, /device:TPU:0, one launch (start us, length us, event | category | flops | bytes accessed | tf_op | source)
XLA Modules:
  0.0 27.2 jit_solution(15018263393132110830)
XLA Ops:
  0.6 25.9 %design_step.1 = (f32[8,16,128]{2,1,0:T(8,128)S(1)}, f32[8,128]{1,0:T(8,128)S(1)}) custom-call(f32[8,16,128]{2,1,0:T(8,128)} %dens_hbm.1, f32[8,16,128]{2,1,0:T(8,128)} %span_hbm.1, f32[9,8,16,128]{3,2,1,0:T(8,128)} %sens_ref.1, f32[9]{0:T(128)} %viol_hbm.1, f32[9]{0:T(128)} %lam0_hbm.1), custom_call_target="tpu_custom_call" | custom-call | tf_op jit(solution)/shard_map/design_step/pallas_call | solution.py:724
  26.6 0.7 %finish.1 = (f32[8,16,128]{2,1,0:T(8,128)}, f32[9]{0:T(128)}) custom-call(f32[8,16,128]{2,1,0:T(8,128)S(1)} %get-tuple-element.4.field_ref, f32[8,128]{1,0:T(8,128)S(1)} %get-tuple-element.5.lam_ref), custom_call_target="tpu_custom_call" | custom-call | tf_op jit(solution)/shard_map/finish/pallas_call | solution.py:772

commit v5 on v4

--- a/solution.py
+++ b/solution.py
@@ -28,6 +28,11 @@
 ROWS = SUMS + FIELDS
 MESH = pl.DeviceIdType.MESH
 GROUP = 3
+KEPT = 2
+
+
+def compact(shape):
+    return shape["gz"] == 2 and shape["gy"] in (2, 4) and shape["gx"] <= 4
 
 
 def plan(shape):
@@ -49,12 +54,12 @@
 
 
 def body(shape, dims, dens_hbm, span_hbm, sens_ref, viol_hbm, lam0_hbm, out_ref, lam_out,
-         dens_ref, span_ref, viol_ref, lam0_ref, pad, xpad, ypack, yrecv, cpack, crecv, ymid,
+         dens_ref, span_ref, dens_more, span_more, viol_ref, lam0_ref, pad, xpad, ypack, yrecv, cpack, crecv, ymid,
          zpack, zrecv, xzpack, xzrecv, yzpack, yzrecv, czrecv, around, mid, invden, pp, qq, slope, scaled,
          acc, wide, lam, part, *rest):
     stages = plan(shape)
     recvs = rest[: len(stages)]
-    load_sem, send_sem, recv_sem, zsend_sem, zrecv_sem, sum_send, sum_recv, known = rest[len(stages):]
+    load_sem, send_sem, recv_sem, zsend_sem, zrecv_sem, lend_send, lend_recv, sum_send, sum_recv, known = rest[len(stages):]
     nx, ny, nz = dims
     tiles = ny // SUB
     chunks = nx * tiles
@@ -103,7 +108,9 @@
         has["gz", -1] = has["gz", 1]
     sides = ((0, 1),) if single else ((0, 1), (1, -1))
     barrier = pltpu.get_barrier_semaphore()
-    near = shape["gz"] == 2 and shape["gy"] <= 4 and shape["gx"] <= 4
+    near = compact(shape)
+    distant = lax.rem(me["gy"], 2) == 0
+    lent = chunks + 3
     if near:
         for o in ring:
             @pl.when(both(o))
@@ -261,6 +268,16 @@
                                   gz=sz, gy=sy))
         moves_z.append(remote(zpack, zrecv.at[i], zsend_sem, zrecv_sem, first, gz=sz))
 
+    lend = [
+        pltpu.make_async_remote_copy(
+            src_ref=src, dst_ref=dst, send_sem=lend_send.at[n], recv_sem=lend_recv.at[n],
+            device_id={"gy": me["gy"] + 1 - 2 * lax.rem(me["gy"], 2)}, device_id_type=MESH)
+        for n, (src, dst) in enumerate([
+            (span_ref.at[pl.ds(KEPT, nx - KEPT)], span_more), (dens_ref.at[pl.ds(KEPT, nx - KEPT)], dens_more),
+            (pp.at[:, pl.ds(KEPT * tiles, chunks - KEPT * tiles)], pp.at[:, pl.ds(lent, chunks - KEPT * tiles)]),
+            (qq.at[:, pl.ds(KEPT * tiles, chunks - KEPT * tiles)], qq.at[:, pl.ds(lent, chunks - KEPT * tiles)])])
+    ] if near else []
+
     def start(moves):
         for send, _, copy in moves:
             pl.when(send)(copy.start)
@@ -317,6 +334,8 @@
 
     for copy in small:
         copy.wait()
+    for copy in lend[:2]:
+        pl.when(distant)(copy.start)
     for n, ref in enumerate((span_ref, dens_ref, invden)):
         packed = zero
         for k in range(chunks):
@@ -394,8 +413,12 @@
         for j in range(FIELDS):
             big_p += weights[j] * pp[j + 1, k]
             big_q += weights[j] * qq[j + 1, k]
-        s = piece(span_ref, k) if k < chunks else around[0, k - chunks]
-        d = piece(dens_ref, k) if k < chunks else around[1, k - chunks]
+        if k >= lent:
+            s, d = piece(span_more, k - lent), piece(dens_more, k - lent)
+        elif k >= chunks:
+            s, d = around[0, k - chunks], around[1, k - chunks]
+        else:
+            s, d = piece(span_ref, k), piece(dens_ref, k)
         root_p = jnp.sqrt(big_p)
         root_q = jnp.sqrt(big_q)
         lower, upper = d - s, d + s
@@ -423,22 +446,22 @@
 
     def main_sums(weights, ks, masked, more):
         grads = [acc[j] if more else zero for j in range(FIELDS)]
-        for k in ks:
+        for n, k in enumerate(ks):
             extra, slopes, ratios = terms(k, weights, keep_of(k) if masked else None)
             for j in range(FIELDS):
                 grads[j] += extra[j]
-                slope[j, k] = slopes[j]
-                scaled[j, k] = ratios[j]
+                slope[j, n] = slopes[j]
+                scaled[j, n] = ratios[j]
         for j in range(FIELDS):
             acc[j] = grads[j]
         at_row = FIELDS
         for group in ((0, 1), (2, 3), (4, 5, 6, 7, 8)):
             keys = [(i, j) for i in group for j in range(i, FIELDS)]
             sums = {key: acc[at_row + n] if more else zero for n, key in enumerate(keys)}
-            for k in ks:
-                right = {j: slope[j, k] for j in range(group[0], FIELDS)}
+            for n in range(len(ks)):
+                right = {j: slope[j, n] for j in range(group[0], FIELDS)}
                 for i in group:
-                    left = scaled[i, k]
+                    left = scaled[i, n]
                     for j in range(i, FIELDS):
                         sums[i, j] += left * right[j]
             for key in keys:
@@ -552,9 +575,15 @@
 
     def between():
         repair()
+        if near:
+            for copy in lend[2:]:
+                pl.when(distant)(copy.start)
         for moves in [moves_c, moves_y] + xs + [moves_z]:
             for send, _, copy in moves:
                 pl.when(send)(copy.wait_send)
+        if near:
+            for copy in lend:
+                pl.when(jnp.logical_not(distant))(copy.wait_recv)
 
     def repair():
         for f in range(FIELDS):
@@ -575,9 +604,9 @@
             index = index * shape[a] + me[a]
         return index
 
-    def exchange(it, meanwhile):
+    def exchange(it, count, meanwhile):
         packed = zero
-        for g in range(wide.shape[0]):
+        for g in range(count):
             values = [acc[r] if r < ROWS else zero for r in range(g * SUB, (g + 1) * SUB)]
             half = SUB // 2
             while half:
@@ -611,7 +640,7 @@
                 values = [sum(values[i + 1 : i + 2], values[i]) for i in range(0, len(values), 2)]
             value = values[0]
         every = jnp.broadcast_to(value, (SUB, LANE))
-        for g in range(wide.shape[0]):
+        for g in range(count):
             one = jnp.sum(jnp.where(lane == g * SUB + row, every, 0.0), axis=1, keepdims=True)
             wide[g] = jnp.broadcast_to(one, (SUB, LANE))
 
@@ -650,8 +679,17 @@
 
     def newton(it, carry):
         weights = [lam[j] for j in range(FIELDS)]
-        main_sums(weights, range(chunks), False, False)
-        exchange(it, lambda: None)
+        if near:
+            @pl.when(distant)
+            def _():
+                main_sums(weights, range(KEPT * tiles), False, False)
+
+            @pl.when(jnp.logical_not(distant))
+            def _():
+                main_sums(weights, list(range(chunks)) + list(range(lent, pp.shape[1])), False, False)
+        else:
+            main_sums(weights, range(chunks), False, False)
+        exchange(it, -(-SUMS // SUB), lambda: None)
         solve(weights)
         return carry
 
@@ -673,14 +711,14 @@
         receive(xs[g])
         for j, f in enumerate(fields):
             inner[g] = rows(f, j, inner[g], faces)
+    receive(moves_z)
     main_sums(weights, faces, True, True)
-    receive(moves_z)
     within = lane < slots
     bases = [jnp.where(within, v, 0.0) for v in edge_rows(extras)]
     extra_sums(weights, (chunks,), within, bases)
     if near:
         pl.semaphore_wait(known.at[1], friends)
-    exchange(0, between)
+    exchange(0, wide.shape[0], between)
     solve(weights)
     lax.fori_loop(1, ITERS, newton, 0)
 
@@ -693,6 +731,8 @@
         final = jnp.where(lane == j, weights[j], final)
     lam_out[...] = final
 
+    for copy in lend:
+        pl.when(distant)(copy.wait_send)
     for it in range(ITERS):
         for n, axes in enumerate(stages):
             size = math.prod(shape[a] for a in axes)
@@ -717,6 +757,8 @@
     stages = plan(shape)
     corners = 9 if shape["gz"] == 2 else 18
     depth = corners // 9
+    more = nx - KEPT if compact(shape) else 1
+    every = chunks + 3 + (more * ny // SUB if compact(shape) else 0)
     f32 = jnp.float32
     vmem = pl.BlockSpec(memory_space=pltpu.VMEM)
     dma = pltpu.SemaphoreType.DMA
@@ -732,6 +774,8 @@
         scratch_shapes=[
             pltpu.VMEM((nx, ny, nz), f32),
             pltpu.VMEM((nx, ny, nz), f32),
+            pltpu.VMEM((more, ny, nz), f32),
+            pltpu.VMEM((more, ny, nz), f32),
             pltpu.SMEM((FIELDS,), f32),
             pltpu.SMEM((FIELDS,), f32),
             pltpu.VMEM((FIELDS, nx, ny + 2 * SUB, nz), f32),
@@ -751,10 +795,10 @@
             pltpu.VMEM((3, 3, SUB, LANE), f32),
             pltpu.VMEM((FIELDS, chunks, SUB, LANE), f32),
             pltpu.VMEM((chunks, SUB, LANE), f32),
-            pltpu.VMEM((FIELDS + 1, chunks + 3, SUB, LANE), f32),
-            pltpu.VMEM((FIELDS + 1, chunks + 3, SUB, LANE), f32),
-            pltpu.VMEM((FIELDS, chunks, SUB, LANE), f32),
-            pltpu.VMEM((FIELDS, chunks, SUB, LANE), f32),
+            pltpu.VMEM((FIELDS + 1, every, SUB, LANE), f32),
+            pltpu.VMEM((FIELDS + 1, every, SUB, LANE), f32),
+            pltpu.VMEM((FIELDS, every, SUB, LANE), f32),
+            pltpu.VMEM((FIELDS, every, SUB, LANE), f32),
             pltpu.VMEM((ROWS, SUB, LANE), f32),
             pltpu.VMEM((-(-ROWS // SUB), SUB, LANE), f32),
             pltpu.VMEM((FIELDS, SUB, LANE), f32),
@@ -762,7 +806,7 @@
         ] + [
             pltpu.VMEM((ITERS, math.prod(shape[a] for a in axes), 1, LANE), f32) for axes in stages
         ] + [
-            dma((5,)), dma((6 + 2 * groups,)), dma((6 + 2 * groups,)), dma((corners,)), dma((corners,)),
+            dma((5,)), dma((6 + 2 * groups,)), dma((6 + 2 * groups,)), dma((corners,)), dma((corners,)), dma((4,)), dma((4,)),
             dma((ITERS, len(stages))), dma((ITERS, len(stages))), pltpu.SemaphoreType.REGULAR((2,)),
         ],
         compiler_params=pltpu.CompilerParams(

time: 27.4 us -> 26.7 us (0.974)
  Pallas kernels: 26.6 us -> 25.9 us
    pallas_call x1, Pallas kernels: 25.9 us -> 25.3 us  [shards(): pl.pallas_call(functools.partial(body, shape, (nx, ny, nz)), out_shape=(p...]
where the time goes in v5:
time: 26.7 us; the launch traced here: 26.6 us
  Pallas kernels  25.9 us (97%)
  between operations  0.64 us (2%)
    pallas_call x1, Pallas kernels, shards(): pl.pallas_call(functools.partial(body, shape, (nx, ny, nz)), out_shape=(p...  25.3 us
    pallas_call x1, Pallas kernels, shards(): pl.pallas_call(finish, out_shape=(jax.ShapeDtypeStruct((nx, ny, nz), f32)...  0.65 us

profile of v5, /device:TPU:0, one launch (start us, length us, event | category | flops | bytes accessed | tf_op | source)
XLA Modules:
  0.0 26.6 jit_solution(18416399947792060708)
XLA Ops:
  0.6 25.3 %design_step.1 = (f32[8,16,128]{2,1,0:T(8,128)S(1)}, f32[8,128]{1,0:T(8,128)S(1)}) custom-call(f32[8,16,128]{2,1,0:T(8,128)} %dens_hbm.1, f32[8,16,128]{2,1,0:T(8,128)} %span_hbm.1, f32[9,8,16,128]{3,2,1,0:T(8,128)} %sens_ref.1, f32[9]{0:T(128)} %viol_hbm.1, f32[9]{0:T(128)} %lam0_hbm.1), custom_call_target="tpu_custom_call" | custom-call | tf_op jit(solution)/shard_map/design_step/pallas_call | solution.py:766
  25.9 0.7 %finish.1 = (f32[8,16,128]{2,1,0:T(8,128)}, f32[9]{0:T(128)}) custom-call(f32[8,16,128]{2,1,0:T(8,128)S(1)} %get-tuple-element.4.field_ref, f32[8,128]{1,0:T(8,128)S(1)} %get-tuple-element.5.lam_ref), custom_call_target="tpu_custom_call" | custom-call | tf_op jit(solution)/shard_map/finish/pallas_call | solution.py:816

commit v6 on v5

--- a/solution.py
+++ b/solution.py
@@ -54,28 +54,19 @@
 
 
 def body(shape, dims, dens_hbm, span_hbm, sens_ref, viol_hbm, lam0_hbm, out_ref, lam_out,
-         dens_ref, span_ref, dens_more, span_more, viol_ref, lam0_ref, pad, xpad, ypack, yrecv, cpack, crecv, ymid,
-         zpack, zrecv, xzpack, xzrecv, yzpack, yzrecv, czrecv, around, mid, invden, pp, qq, slope, scaled,
+         fields_ref, fields_more, viol_ref, lam0_ref, pad, xpad, ypack, yrecv, cpack, crecv, ymid,
+         zpack, zrecv, xzpack, xzrecv, yzpack, yzrecv, czrecv, around, mid, invden, both_pq, slope, scaled,
          acc, wide, lam, part, *rest):
     stages = plan(shape)
     recvs = rest[: len(stages)]
     load_sem, send_sem, recv_sem, zsend_sem, zrecv_sem, lend_send, lend_recv, sum_send, sum_recv, known = rest[len(stages):]
+    pp, qq = both_pq.at[0], both_pq.at[1]
+    span_ref, dens_ref = fields_ref.at[0], fields_ref.at[1]
+    span_more, dens_more = fields_more.at[0], fields_more.at[1]
     nx, ny, nz = dims
     tiles = ny // SUB
     chunks = nx * tiles
     slots = 2 * chunks
-    load = pltpu.make_async_copy(
-        sens_ref, pad.at[:, :, SUB : SUB + ny, :], load_sem.at[0]
-    )
-    load.start()
-    small = [
-        pltpu.make_async_copy(src, dst, load_sem.at[1 + i])
-        for i, (src, dst) in enumerate([
-            (span_hbm, span_ref), (dens_hbm, dens_ref), (viol_hbm, viol_ref), (lam0_hbm, lam0_ref)])
-    ]
-    for copy in small:
-        copy.start()
-    wide_x = 2 * tiles
     groups = steps()
     count_of = len(groups)
     me = {a: lax.axis_index(a) for a in AXES}
@@ -133,6 +124,18 @@
             pl.semaphore_signal(barrier, inc=1, device_id=target, device_id_type=MESH)
         arrivals = len(partners)
 
+    load = pltpu.make_async_copy(
+        sens_ref, pad.at[:, :, SUB : SUB + ny, :], load_sem.at[0]
+    )
+    load.start()
+    small = [
+        pltpu.make_async_copy(src, dst, load_sem.at[1 + i])
+        for i, (src, dst) in enumerate([
+            (span_hbm, span_ref), (dens_hbm, dens_ref), (viol_hbm, viol_ref), (lam0_hbm, lam0_ref)])
+    ]
+    for copy in small:
+        copy.start()
+    wide_x = 2 * tiles
     lane = lax.broadcasted_iota(jnp.int32, (SUB, LANE), 1)
     row = lax.broadcasted_iota(jnp.int32, (SUB, LANE), 0)
     zero = jnp.zeros((SUB, LANE), jnp.float32)
@@ -273,9 +276,9 @@
             src_ref=src, dst_ref=dst, send_sem=lend_send.at[n], recv_sem=lend_recv.at[n],
             device_id={"gy": me["gy"] + 1 - 2 * lax.rem(me["gy"], 2)}, device_id_type=MESH)
         for n, (src, dst) in enumerate([
-            (span_ref.at[pl.ds(KEPT, nx - KEPT)], span_more), (dens_ref.at[pl.ds(KEPT, nx - KEPT)], dens_more),
-            (pp.at[:, pl.ds(KEPT * tiles, chunks - KEPT * tiles)], pp.at[:, pl.ds(lent, chunks - KEPT * tiles)]),
-            (qq.at[:, pl.ds(KEPT * tiles, chunks - KEPT * tiles)], qq.at[:, pl.ds(lent, chunks - KEPT * tiles)])])
+            (fields_ref.at[:, pl.ds(KEPT, nx - KEPT)], fields_more),
+            (both_pq.at[:, :, pl.ds(KEPT * tiles, chunks - KEPT * tiles)],
+             both_pq.at[:, :, pl.ds(lent, chunks - KEPT * tiles)])])
     ] if near else []
 
     def start(moves):
@@ -334,7 +337,7 @@
 
     for copy in small:
         copy.wait()
-    for copy in lend[:2]:
+    for copy in lend[:1]:
         pl.when(distant)(copy.start)
     for n, ref in enumerate((span_ref, dens_ref, invden)):
         packed = zero
@@ -576,14 +579,16 @@
     def between():
         repair()
         if near:
-            for copy in lend[2:]:
+            for copy in lend[1:]:
                 pl.when(distant)(copy.start)
         for moves in [moves_c, moves_y] + xs + [moves_z]:
             for send, _, copy in moves:
                 pl.when(send)(copy.wait_send)
         if near:
-            for copy in lend:
-                pl.when(jnp.logical_not(distant))(copy.wait_recv)
+            @pl.when(jnp.logical_not(distant))
+            def _():
+                for copy in lend:
+                    copy.wait_recv()
 
     def repair():
         for f in range(FIELDS):
@@ -603,6 +608,23 @@
         for a in axes:
             index = index * shape[a] + me[a]
         return index
+
+    def moved(a, d):
+        size = shape[a]
+        if size & (size - 1) or d < 1 or d > 3:
+            return lax.rem(me[a] + d, size)
+        if d == 1:
+            return me[a] + 1 - 2 * lax.rem(me[a], 2)
+        if d == 2:
+            return me[a] + 2 - 4 * lax.rem(me[a] // 2, 2)
+        return me[a] + 3 - 2 * lax.rem(me[a], 4)
+
+    targets = []
+    for axes in stages:
+        to = {(a, d): moved(a, d) if d else me[a] for a in axes for d in range(shape[a])}
+        far = sorted(offsets(axes, shape), reverse=True, key=lambda o: (
+            sum(d // 2 if a == "gy" else d for a, d in zip(axes, o)), [-d for d in o]))
+        targets.append([{a: to[a, d] for a, d in zip(axes, o)} for o in far])
 
     def exchange(it, count, meanwhile):
         packed = zero
@@ -625,11 +647,10 @@
             size = math.prod(shape[a] for a in axes)
             part[it, n] = value
             recvs[n][it, flat(axes)] = value
-            for o in sorted(offsets(axes, shape), key=lambda o: (-abs(o[-1] - 2), o), reverse=True):
-                target = {a: lax.rem(me[a] + d, shape[a]) for a, d in zip(axes, o)}
+            for target in targets[n]:
                 pltpu.make_async_remote_copy(
                     src_ref=part.at[it, n], dst_ref=recvs[n].at[it, flat(axes)],
-                    send_sem=sum_send.at[it, n], recv_sem=sum_recv.at[it, n],
+                    send_sem=sum_send.at[n], recv_sem=sum_recv.at[it, n],
                     device_id=target, device_id_type=MESH).start()
             if n == 0:
                 meanwhile()
@@ -686,7 +707,7 @@
 
             @pl.when(jnp.logical_not(distant))
             def _():
-                main_sums(weights, list(range(chunks)) + list(range(lent, pp.shape[1])), False, False)
+                main_sums(weights, list(range(chunks)) + list(range(lent, both_pq.shape[2])), False, False)
         else:
             main_sums(weights, range(chunks), False, False)
         exchange(it, -(-SUMS // SUB), lambda: None)
@@ -731,13 +752,15 @@
         final = jnp.where(lane == j, weights[j], final)
     lam_out[...] = final
 
-    for copy in lend:
-        pl.when(distant)(copy.wait_send)
-    for it in range(ITERS):
-        for n, axes in enumerate(stages):
-            size = math.prod(shape[a] for a in axes)
-            whole = recvs[n].at[it, pl.ds(0, size - 1)]
-            pltpu.make_async_copy(whole, whole, sum_send.at[it, n]).wait()
+    if near:
+        @pl.when(distant)
+        def _():
+            for copy in lend:
+                copy.wait_send()
+    for n, axes in enumerate(stages):
+        size = math.prod(shape[a] for a in axes)
+        whole = recvs[n].at[:, pl.ds(0, size - 1)]
+        pltpu.make_async_copy(whole, whole, sum_send.at[n]).wait()
 
 
 def finish(field_ref, lam_ref, field_out, lam_out, row, sem):
@@ -772,10 +795,8 @@
         in_specs=[hbm] * 5,
         out_specs=(vmem, vmem),
         scratch_shapes=[
-            pltpu.VMEM((nx, ny, nz), f32),
-            pltpu.VMEM((nx, ny, nz), f32),
-            pltpu.VMEM((more, ny, nz), f32),
-            pltpu.VMEM((more, ny, nz), f32),
+            pltpu.VMEM((2, nx, ny, nz), f32),
+            pltpu.VMEM((2, more, ny, nz), f32),
             pltpu.SMEM((FIELDS,), f32),
             pltpu.SMEM((FIELDS,), f32),
             pltpu.VMEM((FIELDS, nx, ny + 2 * SUB, nz), f32),
@@ -795,8 +816,7 @@
             pltpu.VMEM((3, 3, SUB, LANE), f32),
             pltpu.VMEM((FIELDS, chunks, SUB, LANE), f32),
             pltpu.VMEM((chunks, SUB, LANE), f32),
-            pltpu.VMEM((FIELDS + 1, every, SUB, LANE), f32),
-            pltpu.VMEM((FIELDS + 1, every, SUB, LANE), f32),
+            pltpu.VMEM((2, FIELDS + 1, every, SUB, LANE), f32),
             pltpu.VMEM((FIELDS, every, SUB, LANE), f32),
             pltpu.VMEM((FIELDS, every, SUB, LANE), f32),
             pltpu.VMEM((ROWS, SUB, LANE), f32),
@@ -806,8 +826,8 @@
         ] + [
             pltpu.VMEM((ITERS, math.prod(shape[a] for a in axes), 1, LANE), f32) for axes in stages
         ] + [
-            dma((5,)), dma((6 + 2 * groups,)), dma((6 + 2 * groups,)), dma((corners,)), dma((corners,)), dma((4,)), dma((4,)),
-            dma((ITERS, len(stages))), dma((ITERS, len(stages))), pltpu.SemaphoreType.REGULAR((2,)),
+            dma((5,)), dma((6 + 2 * groups,)), dma((6 + 2 * groups,)), dma((corners,)), dma((corners,)), dma((2,)), dma((2,)),
+            dma((len(stages),)), dma((ITERS, len(stages))), pltpu.SemaphoreType.REGULAR((2,)),
         ],
         compiler_params=pltpu.CompilerParams(
             collective_id=0, has_side_effects=True, vmem_limit_bytes=24 << 20),

time: 26.7 us -> 26.4 us (0.989)
  Pallas kernels: 25.9 us -> 25.6 us
    pallas_call x1, Pallas kernels: 25.3 us -> 24.9 us  [shards(): pl.pallas_call(functools.partial(body, shape, (nx, ny, nz)), out_shape=(p...]
where the time goes in v6:
time: 26.4 us; the launch traced here: 26.2 us
  Pallas kernels  25.6 us (97%)
  between operations  0.64 us (2%)
    pallas_call x1, Pallas kernels, shards(): pl.pallas_call(functools.partial(body, shape, (nx, ny, nz)), out_shape=(p...  24.9 us
    pallas_call x1, Pallas kernels, shards(): pl.pallas_call(finish, out_shape=(jax.ShapeDtypeStruct((nx, ny, nz), f32)...  0.65 us

profile of v6, /device:TPU:0, one launch (start us, length us, event | category | flops | bytes accessed | tf_op | source)
XLA Modules:
  0.0 26.2 jit_solution(14124996696213171668)
XLA Ops:
  0.6 24.9 %design_step.1 = (f32[8,16,128]{2,1,0:T(8,128)S(1)}, f32[8,128]{1,0:T(8,128)S(1)}) custom-call(f32[8,16,128]{2,1,0:T(8,128)} %dens_hbm.1, f32[8,16,128]{2,1,0:T(8,128)} %span_hbm.1, f32[9,8,16,128]{3,2,1,0:T(8,128)} %sens_ref.1, f32[9]{0:T(128)} %viol_hbm.1, f32[9]{0:T(128)} %lam0_hbm.1), custom_call_target="tpu_custom_call" | custom-call | tf_op jit(solution)/shard_map/design_step/pallas_call | solution.py:789
  25.6 0.7 %finish.1 = (f32[8,16,128]{2,1,0:T(8,128)}, f32[9]{0:T(128)}) custom-call(f32[8,16,128]{2,1,0:T(8,128)S(1)} %get-tuple-element.4.field_ref, f32[8,128]{1,0:T(8,128)S(1)} %get-tuple-element.5.lam_ref), custom_call_target="tpu_custom_call" | custom-call | tf_op jit(solution)/shard_map/finish/pallas_call | solution.py:836

commit v7 on v6

--- a/solution.py
+++ b/solution.py
@@ -69,6 +69,12 @@
     slots = 2 * chunks
     groups = steps()
     count_of = len(groups)
+    loads = []
+    for g, fields in enumerate(groups):
+        part_of = pl.ds(fields[0], len(fields))
+        loads.append(pltpu.make_async_copy(
+            sens_ref.at[part_of], pad.at[part_of, :, SUB : SUB + ny, :], load_sem.at[4 + g]))
+        loads[g].start()
     me = {a: lax.axis_index(a) for a in AXES}
 
     has = {}
@@ -124,12 +130,8 @@
             pl.semaphore_signal(barrier, inc=1, device_id=target, device_id_type=MESH)
         arrivals = len(partners)
 
-    load = pltpu.make_async_copy(
-        sens_ref, pad.at[:, :, SUB : SUB + ny, :], load_sem.at[0]
-    )
-    load.start()
     small = [
-        pltpu.make_async_copy(src, dst, load_sem.at[1 + i])
+        pltpu.make_async_copy(src, dst, load_sem.at[i])
         for i, (src, dst) in enumerate([
             (span_hbm, span_ref), (dens_hbm, dens_ref), (viol_hbm, viol_ref), (lam0_hbm, lam0_ref)])
     ]
@@ -197,7 +199,6 @@
             k = x * tiles + t
             invden[k] = 1.0 / den
 
-    load.wait()
 
     def turned(value, shift, axis=1):
         shift %= value.shape[axis]
@@ -207,10 +208,18 @@
         here = lane // 2 == k + j * chunks
         return jnp.where(here, turned(value, 2 * k + 1 + j * slots), packed)
 
+    lines = pad.reshape(FIELDS, nx * (ny + 2 * SUB), nz)
     edges = []
     for g, fields in enumerate(groups):
+        loads[g].wait()
         packed = zero
         for j, f in enumerate(fields):
+            for i, y in enumerate((SUB + ny - 1, SUB)):
+                ypack[i, f] = lines[f, pl.ds(y, nx, stride=ny + 2 * SUB), :]
+            for i, (sx, sy) in enumerate(corners):
+                x = nx - 1 if sx > 0 else 0
+                y = SUB + ny - 1 if sy > 0 else SUB
+                cpack[i, f] = pad[f, x, y : y + 1, :]
             for k in range(chunks):
                 x, t = divmod(k, tiles)
                 packed = place(packed, pad[f, x, SUB + t * SUB : 2 * SUB + t * SUB, :], k, j)
@@ -226,15 +235,6 @@
         for g in range(count_of):
             packed = jnp.where(row == g, jnp.broadcast_to(edges[g][y : y + 1, :], (SUB, LANE)), packed)
         yzpack[n] = packed
-    for f in range(FIELDS):
-        for i, y in enumerate((SUB + ny - 1, SUB)):
-            for x in range(nx):
-                ypack[i, f, x : x + 1, :] = pad[f, x, y : y + 1, :]
-        for i, (sx, sy) in enumerate(corners):
-            x = nx - 1 if sx > 0 else 0
-            y = SUB + ny - 1 if sy > 0 else SUB
-            cpack[i, f] = pad[f, x, y : y + 1, :]
-
     pl.semaphore_wait(barrier, arrivals)
 
     def remote(src, dst, sends, recvs_, index, **moves):
@@ -277,8 +277,8 @@
             device_id={"gy": me["gy"] + 1 - 2 * lax.rem(me["gy"], 2)}, device_id_type=MESH)
         for n, (src, dst) in enumerate([
             (fields_ref.at[:, pl.ds(KEPT, nx - KEPT)], fields_more),
-            (both_pq.at[:, :, pl.ds(KEPT * tiles, chunks - KEPT * tiles)],
-             both_pq.at[:, :, pl.ds(lent, chunks - KEPT * tiles)])])
+            (both_pq.at[:, pl.ds(0, FIELDS), pl.ds(KEPT * tiles, chunks - KEPT * tiles)],
+             both_pq.at[:, pl.ds(0, FIELDS), pl.ds(lent, chunks - KEPT * tiles)])])
     ] if near else []
 
     def start(moves):
@@ -577,31 +577,42 @@
             acc[r] += value
 
     def between():
-        repair()
-        if near:
-            for copy in lend[1:]:
-                pl.when(distant)(copy.start)
+        for fields in groups:
+            for f in fields:
+                repair(f, range(KEPT * tiles, chunks))
+            if near:
+                of, at_k = pl.ds(fields[0], len(fields)), pl.ds(KEPT * tiles, chunks - KEPT * tiles)
+                pl.when(distant)(pltpu.make_async_remote_copy(
+                    src_ref=both_pq.at[:, of, at_k],
+                    dst_ref=both_pq.at[:, of, pl.ds(lent, chunks - KEPT * tiles)],
+                    send_sem=lend_send.at[1], recv_sem=lend_recv.at[1],
+                    device_id={"gy": me["gy"] + 1 - 2 * lax.rem(me["gy"], 2)}, device_id_type=MESH).start)
+        for f in range(FIELDS):
+            repair(f, range(KEPT * tiles))
         for moves in [moves_c, moves_y] + xs + [moves_z]:
             for send, _, copy in moves:
                 pl.when(send)(copy.wait_send)
         if near:
             @pl.when(jnp.logical_not(distant))
             def _():
-                for copy in lend:
-                    copy.wait_recv()
-
-    def repair():
-        for f in range(FIELDS):
-            for ref in (pp, qq):
-                edge = ref[f, chunks]
-                for k in range(chunks):
-                    x, t = divmod(k, tiles)
-                    value = ref[f, k]
-                    for i, y in enumerate((0, ny - 1)):
-                        if t == y // SUB and k in core:
-                            line = jnp.broadcast_to(ref[f, chunks + 1 + i, x : x + 1, :], (SUB, LANE))
-                            value = jnp.where(row == y % SUB, line, value)
-                    ref[f, k] = jnp.where(ends, turned(edge, -2 * k - 1), value)
+                lend[0].wait_recv()
+                for k in range(lent, both_pq.shape[2]):
+                    s = piece(span_more, k - lent)
+                    pp[FIELDS, k] = s * s * (1.001 + RAA)
+                    qq[FIELDS, k] = s * s * (0.001 + RAA)
+                lend[1].wait_recv()
+
+    def repair(f, ks):
+        for ref in (pp, qq):
+            edge = ref[f, chunks]
+            for k in ks:
+                x, t = divmod(k, tiles)
+                value = ref[f, k]
+                for i, y in enumerate((0, ny - 1)):
+                    if t == y // SUB and k in core:
+                        line = jnp.broadcast_to(ref[f, chunks + 1 + i, x : x + 1, :], (SUB, LANE))
+                        value = jnp.where(row == y % SUB, line, value)
+                ref[f, k] = jnp.where(ends, turned(edge, -2 * k - 1), value)
 
     def flat(axes):
         index = 0
@@ -826,7 +837,7 @@
         ] + [
             pltpu.VMEM((ITERS, math.prod(shape[a] for a in axes), 1, LANE), f32) for axes in stages
         ] + [
-            dma((5,)), dma((6 + 2 * groups,)), dma((6 + 2 * groups,)), dma((corners,)), dma((corners,)), dma((2,)), dma((2,)),
+            dma((4 + groups,)), dma((6 + 2 * groups,)), dma((6 + 2 * groups,)), dma((corners,)), dma((corners,)), dma((2,)), dma((2,)),
             dma((len(stages),)), dma((ITERS, len(stages))), pltpu.SemaphoreType.REGULAR((2,)),
         ],
         compiler_params=pltpu.CompilerParams(

time: 26.4 us -> 26.4 us (level)
  no operation moved by 1% of the time
where the time goes in v7:
time: 26.4 us; the launch traced here: 26.2 us
  Pallas kernels  25.6 us (97%)
  between operations  0.64 us (2%)
    pallas_call x1, Pallas kernels, shards(): pl.pallas_call(functools.partial(body, shape, (nx, ny, nz)), out_shape=(p...  24.9 us
    pallas_call x1, Pallas kernels, shards(): pl.pallas_call(finish, out_shape=(jax.ShapeDtypeStruct((nx, ny, nz), f32)...  0.65 us

profile of v7, /device:TPU:0, one launch (start us, length us, event | category | flops | bytes accessed | tf_op | source)
XLA Modules:
  0.0 26.2 jit_solution(603022662981630806)
XLA Ops:
  0.6 24.9 %design_step.1 = (f32[8,16,128]{2,1,0:T(8,128)S(1)}, f32[8,128]{1,0:T(8,128)S(1)}) custom-call(f32[8,16,128]{2,1,0:T(8,128)} %dens_hbm.1, f32[8,16,128]{2,1,0:T(8,128)} %span_hbm.1, f32[9,8,16,128]{3,2,1,0:T(8,128)} %sens_ref.1, f32[9]{0:T(128)} %viol_hbm.1, f32[9]{0:T(128)} %lam0_hbm.1), custom_call_target="tpu_custom_call" | custom-call | tf_op jit(solution)/shard_map/design_step/pallas_call | solution.py:800
  25.6 0.7 %finish.1 = (f32[8,16,128]{2,1,0:T(8,128)}, f32[9]{0:T(128)}) custom-call(f32[8,16,128]{2,1,0:T(8,128)S(1)} %get-tuple-element.4.field_ref, f32[8,128]{1,0:T(8,128)S(1)} %get-tuple-element.5.lam_ref), custom_call_target="tpu_custom_call" | custom-call | tf_op jit(solution)/shard_map/finish/pallas_call | solution.py:847

commit v8 on v7

--- a/solution.py
+++ b/solution.py
@@ -47,6 +47,9 @@
     for a in axes:
         out = [o + (d,) for o in out for d in range(shape[a])]
     return [o for o in out if any(o)]
+
+
+PARTS = (4, 4, 1)
 
 
 def steps():
@@ -245,8 +248,10 @@
         back = both([-moves.get(a, 0) for a in AXES])
         return there, back, copy
 
+    starts = [sum(PARTS[:n]) for n in range(len(PARTS))]
+
     def moves_x(g):
-        fields = pl.ds(groups[g][0], len(groups[g]))
+        fields = pl.ds(starts[g], PARTS[g])
         return [
             remote(pad.at[fields, nx - 1 if sx > 0 else 0, SUB : SUB + ny, :],
                    xpad.at[i, fields, SUB : SUB + ny, :], send_sem, recv_sem, 6 + 2 * g + i, gx=sx)
@@ -298,13 +303,13 @@
                 pl.semaphore_signal(known.at[n], inc=1, device_id=at(gy=o[1], gx=o[2]),
                                     device_id_type=MESH)
 
-    xs = [moves_x(g) for g in range(count_of)]
+    xs = [moves_x(g) for g in range(len(PARTS))]
     start(moves_z)
     start(moves_c)
     start(xs[0])
     start(moves_y)
-    for g in range(1, count_of):
-        start(xs[g])
+    for move in xs[1:]:
+        start(move)
     if near:
         tell(0)
 
@@ -739,11 +744,13 @@
     receive(moves_c)
     extras, bases = face_rows()
     extra_sums(weights, (chunks + 1, chunks + 2), body_rows, bases)
-    for g, fields in enumerate(groups):
-        receive(xs[g])
-        for j, f in enumerate(fields):
+    for n, move in enumerate(xs):
+        receive(move)
+        if n == len(xs) - 1:
+            receive(moves_z)
+        for f in range(starts[n], starts[n] + PARTS[n]):
+            g, j = divmod(f, GROUP)
             inner[g] = rows(f, j, inner[g], faces)
-    receive(moves_z)
     main_sums(weights, faces, True, True)
     within = lane < slots
     bases = [jnp.where(within, v, 0.0) for v in edge_rows(extras)]
@@ -837,7 +844,7 @@
         ] + [
             pltpu.VMEM((ITERS, math.prod(shape[a] for a in axes), 1, LANE), f32) for axes in stages
         ] + [
-            dma((4 + groups,)), dma((6 + 2 * groups,)), dma((6 + 2 * groups,)), dma((corners,)), dma((corners,)), dma((2,)), dma((2,)),
+            dma((4 + groups,)), dma((6 + 2 * len(PARTS),)), dma((6 + 2 * len(PARTS),)), dma((corners,)), dma((corners,)), dma((2,)), dma((2,)),
             dma((len(stages),)), dma((ITERS, len(stages))), pltpu.SemaphoreType.REGULAR((2,)),
         ],
         compiler_params=pltpu.CompilerParams(

time: 26.4 us -> 26.3 us (level)
  no operation moved by 1% of the time
where the time goes in v8:
time: 26.3 us; the launch traced here: 26.1 us
  Pallas kernels  25.5 us (97%)
  between operations  0.64 us (2%)
    pallas_call x1, Pallas kernels, shards(): pl.pallas_call(functools.partial(body, shape, (nx, ny, nz)), out_shape=(p...  24.8 us
    pallas_call x1, Pallas kernels, shards(): pl.pallas_call(finish, out_shape=(jax.ShapeDtypeStruct((nx, ny, nz), f32)...  0.65 us

profile of v8, /device:TPU:0, one launch (start us, length us, event | category | flops | bytes accessed | tf_op | source)
XLA Modules:
  0.0 26.1 jit_solution(2189260087394685464)
XLA Ops:
  0.6 24.8 %design_step.1 = (f32[8,16,128]{2,1,0:T(8,128)S(1)}, f32[8,128]{1,0:T(8,128)S(1)}) custom-call(f32[8,16,128]{2,1,0:T(8,128)} %dens_hbm.1, f32[8,16,128]{2,1,0:T(8,128)} %span_hbm.1, f32[9,8,16,128]{3,2,1,0:T(8,128)} %sens_ref.1, f32[9]{0:T(128)} %viol_hbm.1, f32[9]{0:T(128)} %lam0_hbm.1), custom_call_target="tpu_custom_call" | custom-call | tf_op jit(solution)/shard_map/design_step/pallas_call | solution.py:807
  25.5 0.7 %finish.1 = (f32[8,16,128]{2,1,0:T(8,128)}, f32[9]{0:T(128)}) custom-call(f32[8,16,128]{2,1,0:T(8,128)S(1)} %get-tuple-element.4.field_ref, f32[8,128]{1,0:T(8,128)S(1)} %get-tuple-element.5.lam_ref), custom_call_target="tpu_custom_call" | custom-call | tf_op jit(solution)/shard_map/finish/pallas_call | solution.py:854
